TPU v7x, 256 devices: a whole 4x4x8 slice. The times are simulated.
256 devices in a mesh: seg: 256 (over x, z, y, core).
Axes of the slice: x: 4, y: 4, z: 8, core: 2. Of those that a mesh axis runs over, the one named last changes fastest.
Arguments:
- cam_jac: bfloat16 [18, 4096, 512], P(None, 'seg'), may hold values from -0.25 to 0.25
- point_jac: bfloat16 [6, 4096, 512], P(None, 'seg'), may hold values from -6 to 6
- obs_point: int32 [4096, 512], P('seg'), may hold values from 0 to 1791, as said below
- obs_count: int32 [4096], P('seg'), may hold values from 64 to 512, as said below
- back_list: int32 [256, 384], P('seg'), may hold values from 0 to 1023, as said below
- front_list: int32 [256, 384], P('seg'), may hold values from 0 to 1023, as said below
- point_damp: float32 [262144], P('seg'), may hold values from 0.5 to 4
- cam_damp: float32 [4096], P('seg'), may hold values from 0.1 to 1
- right_side: float32 [9, 4096], P(None, 'seg'), may hold values from -25 to 25
- start_guess: float32 [9, 4096], P(None, 'seg'), may hold values from -3 to 3
Outputs:
- camera_step: float32 [9, 4096], P(None, 'seg')
- residual: float32 [9, 4096], P(None, 'seg')
Inputs may be any that keep to these rules, and one draw needn't show every extreme that they name: `obs_point`: entries below 1024 name the segment's own points; an entry e from 1024 to 1407 names entry e - 1024 of the previous segment's back_list, and a larger one entry e - 1408 of the next segment's front_list. Keyframes of the first segment name no back slot, those of the last segment no front slot. `obs_count`: slots at or past a keyframe's count are padding. Every segment has a keyframe whose slots are all used. `back_list`: each row holds 384 distinct own points of the segment; no point stands on both lists of its segment. `front_list`: each row holds 384 distinct own points of the segment; no point stands on both lists of its segment.
All inputs are finite; a program needn't handle non-finite values.
Results may differ from a plain program's by a relative error of at most 0.0005.
Values sent between devices are 32-bit elements; how exact they have to be, the bound alone decides.
A program may use at most 64 MiB of HBM per device.

v0:
```python
import jax
import jax.numpy as jnp
from jax import lax
from jax.sharding import Mesh
from jax.sharding import PartitionSpec as P

ITERS = 2
SEG = ("seg_0", "seg_1", "seg_2", "seg_3")


ENTRY_PAIRS = ((0, 0), (0, 1), (0, 2), (1, 1), (1, 2), (2, 2))


def padded(block, sides, width):
    for axis, dim in sides:
        count = lax.axis_size(axis)
        forward = [(i, i + 1) for i in range(count - 1)]
        backward = [(target, source) for source, target in forward]
        low = lax.ppermute(
            lax.slice_in_dim(block, block.shape[dim] - width, None, axis=dim), axis, forward
        )
        high = lax.ppermute(lax.slice_in_dim(block, 0, width, axis=dim), axis, backward)
        block = jnp.concatenate([low, block, high], axis=dim)
    return block


def by_axis(shard, axes):
    for axis in axes:
        shard = lax.psum(shard, axis)
    return shard


def slot_weights(obs_count, slot_total):
    positions = lax.broadcasted_iota(jnp.int32, (obs_count.shape[0], slot_total), 1)
    return (positions < obs_count[:, None]).astype(jnp.float32)


def symmetric_inverse(entries):
    cofactors = [
        entries[3] * entries[5] - entries[4] * entries[4],
        entries[2] * entries[4] - entries[1] * entries[5],
        entries[1] * entries[4] - entries[2] * entries[3],
        entries[0] * entries[5] - entries[2] * entries[2],
        entries[1] * entries[2] - entries[0] * entries[4],
        entries[0] * entries[3] - entries[1] * entries[1],
    ]
    determinant = entries[0] * cofactors[0] + entries[1] * cofactors[1] + entries[2] * cofactors[2]
    determinant = jnp.where(determinant > 0.0, determinant, 1.0)
    return jnp.stack([member / determinant for member in cofactors])


def apply_inverse(inverse, point_sums):
    return jnp.stack(
        [
            inverse[0] * point_sums[0] + inverse[1] * point_sums[1] + inverse[2] * point_sums[2],
            inverse[1] * point_sums[0] + inverse[3] * point_sums[1] + inverse[4] * point_sums[2],
            inverse[2] * point_sums[0] + inverse[4] * point_sums[1] + inverse[5] * point_sums[2],
        ]
    )


def camera_rows(cam_jac, vector, weights):
    error_rows = []
    for row_index in range(2):
        running = cam_jac[9 * row_index].astype(jnp.float32) * vector[0][:, None]
        for column in range(1, 9):
            running = (
                running
                + cam_jac[9 * row_index + column].astype(jnp.float32) * vector[column][:, None]
            )
        error_rows.append(running * weights)
    return error_rows


def both_outgoing(own_sums, slot_sums, back_ids, front_ids, border):
    return jnp.concatenate(
        [
            slot_sums[:, :border],
            own_sums[:, front_ids],
            own_sums[:, back_ids],
            slot_sums[:, border:],
        ],
        axis=1,
    )


def fold_both(own_sums, slot_sums, received, back_ids, front_ids, border):
    from_before = received[:, : 2 * border]
    from_after = received[:, 6 * border :]
    own_complete = (
        own_sums.at[:, front_ids]
        .add(from_before[:, border:])
        .at[:, back_ids]
        .add(from_after[:, :border])
    )
    back_complete = slot_sums[:, :border] + from_before[:, :border]
    front_complete = slot_sums[:, border:] + from_after[:, border:]
    return jnp.concatenate([own_complete, back_complete, front_complete], axis=1)


def shards(
    cam_jac,
    point_jac,
    obs_point,
    obs_count,
    back_list,
    front_list,
    point_damp,
    cam_damp,
    right_side,
    start_guess,
):
    cameras, slot_total = obs_point.shape
    points = point_damp.shape[0]
    border = back_list.shape[1]
    extended = points + 2 * border
    weights = slot_weights(obs_count, slot_total)
    owners = obs_point.reshape(-1)
    back_ids = back_list[0]
    front_ids = front_list[0]
    partial_value = []
    damping = []
    for lead_index, tail_index in ENTRY_PAIRS:
        product = point_jac[lead_index].astype(jnp.float32) * point_jac[tail_index].astype(
            jnp.float32
        )
        product = product + point_jac[3 + lead_index].astype(jnp.float32) * point_jac[
            3 + tail_index
        ].astype(jnp.float32)
        partial_value.append(
            jax.ops.segment_sum((product * weights).reshape(-1), owners, num_segments=extended)
        )
        damping.append(point_damp if lead_index == tail_index else jnp.zeros_like(point_damp))
    partial_value = jnp.stack(partial_value)
    own_part = partial_value[:, :points] + jnp.stack(damping)
    outgoing = both_outgoing(own_part, partial_value[:, points:], back_ids, front_ids, border)
    received = padded(outgoing, ((SEG, 1),), 2 * border)
    inverse = symmetric_inverse(
        fold_both(own_part, partial_value[:, points:], received, back_ids, front_ids, border)
    )
    diagonal = []
    for column in range(9):
        squared = (
            cam_jac[column].astype(jnp.float32) ** 2 + cam_jac[9 + column].astype(jnp.float32) ** 2
        )
        diagonal.append(jnp.sum(squared * weights, axis=1) + cam_damp)
    precond = 1.0 / jnp.stack(diagonal)

    def operator(vector):
        errors = camera_rows(cam_jac, vector, weights)
        point_sums = []
        for column in range(3):
            product = errors[0] * point_jac[column].astype(jnp.float32) + errors[1] * point_jac[
                3 + column
            ].astype(jnp.float32)
            point_sums.append(
                jax.ops.segment_sum(product.reshape(-1), owners, num_segments=extended)
            )
        point_sums = jnp.stack(point_sums)
        outgoing = both_outgoing(
            point_sums[:, :points], point_sums[:, points:], back_ids, front_ids, border
        )
        received = padded(outgoing, ((SEG, 1),), 2 * border)
        values = apply_inverse(
            inverse,
            fold_both(
                point_sums[:, :points],
                point_sums[:, points:],
                received,
                back_ids,
                front_ids,
                border,
            ),
        )
        picked = values[:, owners].reshape(3, cameras, slot_total)
        adjusted = []
        for row_index in range(2):
            back_term = picked[0] * point_jac[3 * row_index].astype(jnp.float32)
            back_term = back_term + picked[1] * point_jac[3 * row_index + 1].astype(jnp.float32)
            back_term = back_term + picked[2] * point_jac[3 * row_index + 2].astype(jnp.float32)
            adjusted.append(errors[row_index] - weights * back_term)
        result = []
        for column in range(9):
            running = jnp.sum(
                cam_jac[column].astype(jnp.float32) * adjusted[0]
                + cam_jac[9 + column].astype(jnp.float32) * adjusted[1],
                axis=1,
            )
            result.append(cam_damp * vector[column] + running)
        return jnp.stack(result)

    def paired(residual, scaled, image):
        return (by_axis(jnp.sum(residual * scaled), SEG), by_axis(jnp.sum(image * scaled), SEG))

    solution = start_guess
    residual = right_side - operator(solution)
    scaled = precond * residual
    image = operator(scaled)
    inner_now, curvature = paired(residual, scaled, image)
    step_size = inner_now / curvature
    direction = scaled
    image_dir = image
    for iteration in range(ITERS):
        solution = solution + step_size * direction
        residual = residual - step_size * image_dir
        if iteration + 1 < ITERS:
            scaled = precond * residual
            image = operator(scaled)
            inner_next, curvature = paired(residual, scaled, image)
            ratio = inner_next / inner_now
            step_size = inner_next / (curvature - ratio * inner_next / step_size)
            direction = scaled + ratio * direction
            image_dir = image + ratio * image_dir
            inner_now = inner_next
    return (solution, residual)


def solution(mesh):
    finer = Mesh(mesh.devices.reshape(4, 8, 4, 2), ("seg_0", "seg_1", "seg_2", "seg_3"))
    return jax.shard_map(
        shards,
        mesh=finer,
        in_specs=(
            P(None, SEG, None),
            P(None, SEG, None),
            P(SEG, None),
            P(SEG),
            P(SEG, None),
            P(SEG, None),
            P(SEG),
            P(SEG),
            P(None, SEG),
            P(None, SEG),
        ),
        out_specs=(P(None, SEG), P(None, SEG)),
        check_vma=False,
    )
```

profile of v0, /device:TPU:1, one launch (start us, length us, event | category | flops | bytes accessed | tf_op | source)
XLA Modules:
  0.0 966.2 jit_solution(1326516934796482926)
XLA Ops:
  6.1 43.6 %scatter_custom_fusion.5 = f32[1792]{0:T(1024)S(1)} fusion(s32[8192]{0:T(1024)S(1)} %bitcast.1428, f32[8192]{0:T(1024)S(1)} %get-tuple-element.138, f32[]{:T(128)} %constant.37.clone.1), kind=kCustom, calls=%fused_computation.547 | custom fusion | flops 8192 | bytes 7172 | tf_op jit(solution)/shard_map/scatter-add | solution.py:131
  49.8 43.6 %scatter_custom_fusion.4 = f32[1792]{0:T(1024)S(1)} fusion(s32[8192]{0:T(1024)S(1)} %bitcast.1429, f32[8192]{0:T(1024)S(1)} %get-tuple-element.139, f32[]{:T(128)} %constant.37.clone.1), kind=kCustom, calls=%fused_computation.549 | custom fusion | flops 8192 | bytes 7172 | tf_op jit(solution)/shard_map/scatter-add | solution.py:131
  93.5 43.6 %scatter_custom_fusion.3 = f32[1792]{0:T(1024)S(1)} fusion(s32[8192]{0:T(1024)S(1)} %bitcast.1430, f32[8192]{0:T(1024)S(1)} %get-tuple-element.140, f32[]{:T(128)} %constant.37.clone.1), kind=kCustom, calls=%fused_computation.551 | custom fusion | flops 8192 | bytes 7172 | tf_op jit(solution)/shard_map/scatter-add | solution.py:131
  137.1 43.6 %scatter_custom_fusion.1 = f32[1792]{0:T(1024)S(1)} fusion(s32[8192]{0:T(1024)S(1)} %bitcast.1431, f32[8192]{0:T(1024)S(1)} %get-tuple-element.141, f32[]{:T(128)} %constant.37.clone.1), kind=kCustom, calls=%fused_computation.555 | custom fusion | flops 8192 | bytes 7172 | tf_op jit(solution)/shard_map/scatter-add | solution.py:131
  180.8 43.6 %scatter_custom_fusion.2 = f32[1792]{0:T(1024)S(1)} fusion(s32[8192]{0:T(1024)S(1)} %bitcast.1432, f32[8192]{0:T(1024)S(1)} %get-tuple-element.142, f32[]{:T(128)} %constant.37.clone.1), kind=kCustom, calls=%fused_computation.553 | custom fusion | flops 8192 | bytes 7172 | tf_op jit(solution)/shard_map/scatter-add | solution.py:131
  224.5 43.6 %scatter_custom_fusion = f32[1792]{0:T(1024)S(1)} fusion(s32[8192]{0:T(1024)S(1)} %bitcast.1433, f32[8192]{0:T(1024)S(1)} %get-tuple-element.143, f32[]{:T(128)} %constant.37.clone.1), kind=kCustom, calls=%fused_computation.557 | custom fusion | flops 8192 | bytes 7172 | tf_op jit(solution)/shard_map/scatter-add | solution.py:131
  270.1 19.5 %collective-permute-start.1 = (f32[6,768]{1,0:T(8,128)S(1)}, f32[6,768]{1,0:T(8,128)S(1)}, u32[]{:S(2)}, u32[]{:S(2)}) collective-permute-start(f32[6,768]{1,0:T(8,128)S(1)} %pad_maximum_fusion.7), channel_id=1, source_target_pairs={{1,0},{2,1},{3,2},{4,3},{5,4},{6,5},{7,6},{8,7},{9,8},{10,9},{11,1... | collective-permute-start | bytes 55304 | tf_op jit(solution)/shard_map/ppermute | solution.py:22
  292.9 43.6 %scatter_custom_fusion.8 = f32[1792]{0:T(1024)S(1)} fusion(s32[8192]{0:T(1024)S(1)} %bitcast.1434, f32[8192]{0:T(1024)S(1)} %get-tuple-element.111, f32[]{:T(128)} %constant.37.clone.1), kind=kCustom, calls=%fused_computation.545 | custom fusion | flops 8192 | bytes 7172 | tf_op jit(solution)/shard_map/scatter-add | solution.py:157
  336.5 44.2 %scatter_custom_fusion.9 = f32[1792]{0:T(1024)S(1)} fusion(s32[8192]{0:T(1024)S(1)} %bitcast.1435, f32[8192]{0:T(1024)S(1)} %get-tuple-element.144, f32[]{:T(128)} %constant.37.clone.1), kind=kCustom, calls=%fused_computation.543 | custom fusion | flops 8192 | bytes 7172 | tf_op jit(solution)/shard_map/scatter-add | solution.py:157
  380.7 43.6 %scatter_custom_fusion.10 = f32[1792]{0:T(1024)S(1)} fusion(s32[8192]{0:T(1024)S(1)} %bitcast.1436, f32[8192]{0:T(1024)S(1)} %get-tuple-element.145, f32[]{:T(128)} %constant.37.clone.1), kind=kCustom, calls=%fused_computation.541 | custom fusion | flops 8192 | bytes 7172 | tf_op jit(solution)/shard_map/scatter-add | solution.py:157
  451.7 27.7 %gather_fusion.4 = f32[8192,3]{1,0:T(8,128)} fusion(f32[3,1792]{0,1:T(8,128)S(1)} %copy.43, s32[8192]{0:T(1024)S(1)} %broadcast_clamp_fusion), kind=kCustom, calls=%fused_computation.4 | custom fusion | bytes 229376 | tf_op jit(solution)/shard_map/gather | solution.py:175
  479.5 10.2 %slice_reduce_fusion.6 = (f32[8192]{0:T(1024)S(1)}, f32[8192]{0:T(1024)S(1)}, f32[8192]{0:T(1024)S(1)}) fusion(f32[3,8192]{0,1:T(8,128)} %bitcast.1306), kind=kLoop, calls=%fused_computation.40 | loop fusion | bytes 196608 | tf_op jit(solution)/shard_map/slice | solution.py:180
  491.1 43.6 %scatter_custom_fusion.13 = f32[1792]{0:T(1024)S(1)} fusion(s32[8192]{0:T(1024)S(1)} %bitcast.1437, f32[8192]{0:T(1024)S(1)} %get-tuple-element.83, f32[]{:T(128)} %constant.37.clone.1), kind=kCustom, calls=%fused_computation.539 | custom fusion | flops 8192 | bytes 7172 | tf_op jit(solution)/shard_map/scatter-add | solution.py:157
  534.8 43.6 %scatter_custom_fusion.14 = f32[1792]{0:T(1024)S(1)} fusion(s32[8192]{0:T(1024)S(1)} %bitcast.1438, f32[8192]{0:T(1024)S(1)} %get-tuple-element.148, f32[]{:T(128)} %constant.37.clone.1), kind=kCustom, calls=%fused_computation.537 | custom fusion | flops 8192 | bytes 7172 | tf_op jit(solution)/shard_map/scatter-add | solution.py:157
  578.5 43.6 %scatter_custom_fusion.15 = f32[1792]{0:T(1024)S(1)} fusion(s32[8192]{0:T(1024)S(1)} %bitcast.1439, f32[8192]{0:T(1024)S(1)} %get-tuple-element.149, f32[]{:T(128)} %constant.37.clone.1), kind=kCustom, calls=%fused_computation.535 | custom fusion | flops 8192 | bytes 7172 | tf_op jit(solution)/shard_map/scatter-add | solution.py:157
  641.6 27.7 %gather_fusion.7 = f32[8192,3]{1,0:T(8,128)} fusion(f32[3,1792]{0,1:T(8,128)S(1)} %copy.50, s32[8192]{0:T(1024)S(1)} %broadcast_clamp_fusion), kind=kCustom, calls=%fused_computation.7 | custom fusion | bytes 229376 | tf_op jit(solution)/shard_map/gather | solution.py:175
  687.3 11.3 %all-reduce.1 = (f32[]{:T(128)}, f32[]{:T(128)}) all-reduce(f32[]{:T(128)} %get-tuple-element.58, f32[]{:T(128)} %get-tuple-element.59), channel_id=1, replica_groups=mesh['seg_0'=4,'seg_1'=8,'seg_2'=4,'seg_3'=2] {'seg_1'}, use_global_device_ids=true, to_apply=%region_33.34 | all-reduce | flops 2 | bytes 16 | tf_op jit(solution)/shard_map/psum | solution.py:29
  698.6 21.6 %all-reduce.3 = (f32[]{:T(128)}, f32[]{:T(128)}) all-reduce(f32[]{:T(128)} %get-tuple-element.50, f32[]{:T(128)} %get-tuple-element.51), channel_id=1, replica_groups=mesh['seg_0'=4,'seg_1'=8,'seg_2'=4,'seg_3'=2] {'seg_2'}, use_global_device_ids=true, to_apply=%region_34.35 | all-reduce | flops 2 | bytes 16 | tf_op jit(solution)/shard_map/psum | solution.py:29
  720.2 10.6 %all-reduce.7 = (f32[]{:T(128)}, f32[]{:T(128)}) all-reduce(f32[]{:T(128)} %get-tuple-element.54, f32[]{:T(128)} %get-tuple-element.55), channel_id=1, replica_groups=mesh['seg_0'=4,'seg_1'=8,'seg_2'=4,'seg_3'=2] {'seg_3'}, use_global_device_ids=true, to_apply=%region_35.36 | all-reduce | flops 2 | bytes 16 | tf_op jit(solution)/shard_map/psum | solution.py:29
  733.0 43.9 %scatter_custom_fusion.18 = f32[1792]{0:T(1024)S(1)} fusion(s32[8192]{0:T(1024)S(1)} %bitcast.1440, f32[8192]{0:T(1024)S(1)} %get-tuple-element.72, f32[]{:T(128)} %constant.37.clone.1), kind=kCustom, calls=%fused_computation.533 | custom fusion | flops 8192 | bytes 7172 | tf_op jit(solution)/shard_map/scatter-add | solution.py:157
  777.0 43.6 %scatter_custom_fusion.19 = f32[1792]{0:T(1024)S(1)} fusion(s32[8192]{0:T(1024)S(1)} %bitcast.1441, f32[8192]{0:T(1024)S(1)} %get-tuple-element.146, f32[]{:T(128)} %constant.37.clone.1), kind=kCustom, calls=%fused_computation.531 | custom fusion | flops 8192 | bytes 7172 | tf_op jit(solution)/shard_map/scatter-add | solution.py:157
  820.6 43.6 %scatter_custom_fusion.20 = f32[1792]{0:T(1024)S(1)} fusion(s32[8192]{0:T(1024)S(1)} %bitcast.1442, f32[8192]{0:T(1024)S(1)} %get-tuple-element.147, f32[]{:T(128)} %constant.37.clone.1), kind=kCustom, calls=%fused_computation.529 | custom fusion | flops 8192 | bytes 7172 | tf_op jit(solution)/shard_map/scatter-add | solution.py:157
  884.8 27.7 %gather_fusion.10 = f32[8192,3]{1,0:T(8,128)} fusion(f32[3,1792]{0,1:T(8,128)S(1)} %copy.57, s32[8192]{0:T(1024)S(1)} %broadcast_clamp_fusion), kind=kCustom, calls=%fused_computation.10 | custom fusion | bytes 229376 | tf_op jit(solution)/shard_map/gather | solution.py:175
  930.6 11.4 %all-reduce = (f32[]{:T(128)}, f32[]{:T(128)}) all-reduce(f32[]{:T(128)} %get-tuple-element.56, f32[]{:T(128)} %get-tuple-element.57), channel_id=1, replica_groups=mesh['seg_0'=4,'seg_1'=8,'seg_2'=4,'seg_3'=2] {'seg_1'}, use_global_device_ids=true, to_apply=%region_57.58 | all-reduce | flops 2 | bytes 16 | tf_op jit(solution)/shard_map/psum | solution.py:29
  (266 shorter events, 134.5 us)
Async XLA Ops:
  0.6 267.6 %copy-start.8 = (s32[1,384]{1,0:T(1,128)S(1)}, s32[1,384]{1,0:T(1,128)}, u32[]{:S(2)}) copy-start(s32[1,384]{1,0:T(1,128)} %param.15) | copy-start | bytes 4612
  0.6 267.7 %copy-start.4 = (f32[1024]{0:T(1024)S(1)}, f32[1024]{0:T(1024)}, u32[]{:S(2)}) copy-start(f32[1024]{0:T(1024)} %param.16) | copy-start | bytes 12292
  3.5 286.2 %copy-start.9 = (s32[1,384]{1,0:T(1,128)S(1)}, s32[1,384]{1,0:T(1,128)}, u32[]{:S(2)}) copy-start(s32[1,384]{1,0:T(1,128)} %param.14) | copy-start | bytes 4612
  4.6 423.3 %copy-start = (bf16[18,16,512]{2,1,0:T(8,128)(2,1)S(1)}, bf16[18,16,512]{2,1,0:T(8,128)(2,1)}, u32[]{:S(2)}) copy-start(bf16[18,16,512]{2,1,0:T(8,128)(2,1)} %param.10) | copy-start | bytes 884740
  4.6 423.3 %copy-start.5 = (s32[16]{0:T(128)S(1)}, s32[16]{0:T(128)}, u32[]{:S(2)}) copy-start(s32[16]{0:T(128)} %param.13) | copy-start | bytes 196
  5.6 422.6 %copy-start.2 = (s32[16,512]{1,0:T(8,128)S(1)}, s32[16,512]{1,0:T(8,128)}, u32[]{:S(2)}) copy-start(s32[16,512]{1,0:T(8,128)} %param.12) | copy-start | bytes 98308
  5.6 422.7 %copy-start.7 = (f32[16]{0:T(128)S(1)}, f32[16]{0:T(128)}, u32[]{:S(2)}) copy-start(f32[16]{0:T(128)} %param.17) | copy-start | bytes 196
  270.1 171.5 %collective-permute-start.1 = (f32[6,768]{1,0:T(8,128)S(1)}, f32[6,768]{1,0:T(8,128)S(1)}, u32[]{:S(2)}, u32[]{:S(2)}) collective-permute-start(f32[6,768]{1,0:T(8,128)S(1)} %pad_maximum_fusion.7), channel_id=1, source_target_pairs={{1,0},{2,1},{3,2},{4,3},{5,4},{6,5},{7,6},{8,7},{9,8},{10,9},{11,1... | collective-permute-start | bytes 55304 | tf_op jit(solution)/shard_map/ppermute | solution.py:22
  290.9 150.7 %collective-permute-start = (f32[6,768]{1,0:T(8,128)S(1)}, f32[6,768]{1,0:T(8,128)S(1)}, u32[]{:S(2)}, u32[]{:S(2)}) collective-permute-start(f32[6,768]{1,0:T(8,128)S(1)} %pad_maximum_fusion.6), channel_id=1, source_target_pairs={{0,1},{1,2},{2,3},{3,4},{4,5},{5,6},{6,7},{7,8},{8,9},{9,10},{10,1... | collective-permute-start | bytes 55304 | tf_op jit(solution)/shard_map/ppermute | solution.py:19
  425.9 9.6 collective-permute-start.2
  435.6 12.2 %collective-permute-start.3 = (f32[3,768]{1,0:T(4,128)S(1)}, f32[3,768]{1,0:T(4,128)S(1)}, u32[]{:S(2)}, u32[]{:S(2)}) collective-permute-start(f32[3,768]{1,0:T(4,128)S(1)} %pad_maximum_fusion.9), channel_id=1, source_target_pairs={{1,0},{2,1},{3,2},{4,3},{5,4},{6,5},{7,6},{8,7},{9,8},{10,9},{11,1... | collective-permute-start | bytes 27656 | tf_op jit(solution)/shard_map/ppermute | solution.py:22
  479.4 10.2 %copy-start.1 = (bf16[6,16,512]{2,1,0:T(8,128)(2,1)S(1)}, bf16[6,16,512]{2,1,0:T(8,128)(2,1)}, u32[]{:S(2)}) copy-start(bf16[6,16,512]{2,1,0:T(8,128)(2,1)} %param.11) | copy-start | bytes 294916
  479.4 10.7 %copy-start.3 = (f32[9,16]{1,0:T(8,128)S(1)}, f32[9,16]{1,0:T(8,128)}, u32[]{:S(2)}) copy-start(f32[9,16]{1,0:T(8,128)} %param.19) | copy-start | bytes 1732
  479.5 10.8 %copy-start.6 = (f32[9,16]{1,0:T(8,128)S(1)}, f32[9,16]{1,0:T(8,128)}, u32[]{:S(2)}) copy-start(f32[9,16]{1,0:T(8,128)} %param.18) | copy-start | bytes 1732
  623.7 8.5 collective-permute-start.4
  632.3 5.7 collective-permute-start.5
  865.8 9.5 collective-permute-start.6
  875.4 5.5 collective-permute-start.7
where the time goes:
time: 973 us; the launch traced here: 966 us
  other arithmetic  687 us (71%)
  local copies, waits for them, and re-layouts  132 us (14%)
  blocking collectives  86.1 us (9%)
  starting transfers between devices  35.7 us (4%)
  waiting for transfers between devices  17.3 us (2%)
    scatter-add x9, other arithmetic, operator(): jax.ops.segment_sum(product.reshape(-1), owners, num_segments=extended)  394 us
    scatter-add x6, other arithmetic, shards(): jax.ops.segment_sum((product * weights).reshape(-1), owners, num_segments...  262 us
    psum x8, blocking collectives, by_axis(): shard = lax.psum(shard, axis)  86.1 us
    gather x3, local copies, waits for them, and re-layouts, operator(): picked = values[:, owners].reshape(3, cameras, slot_total)  83.1 us
    slice x3, local copies, waits for them, and re-layouts, operator(): picked[2] * point_jac[3 * row_index + 2].astype(jnp.float32)  30.5 us
    ppermute x4, starting transfers between devices, padded(): lax.ppermute(lax.slice_in_dim(block, 0, width, axis=dim), axis, backward)  27.6 us
    scatter-add x8, other arithmetic, fold_both(): own_complete = own_sums.at[:, front_ids].add(from_before[:, border:]).at[...  23.3 us
  transfers between devices with their start and end apart: 8, of which 3 were waited for; matrix products, arithmetic and copies ran while one was open for 16% of the time, Pallas kernels for 0%

commit v1 on v0

v1 whole, which is shorter than its diff:
```python
import functools

import jax
import jax.numpy as jnp
from jax import lax
from jax.experimental import pallas as pl
from jax.experimental.pallas import tpu as pltpu
from jax.sharding import PartitionSpec as P

DIMS = (4, 8, 4, 2)
PAIRS = ((0, 0), (0, 1), (0, 2), (1, 1), (1, 2), (2, 2))
F32 = jnp.float32
BF16 = jnp.bfloat16
MESH = pl.DeviceIdType.MESH


def spread(block, rows):
    return jnp.broadcast_to(block, (rows, block.shape[1]))


def lane_pick(row, index):
    return jnp.take_along_axis(row, index, axis=1, mode="promise_in_bounds")


def recip(value):
    first = 1.0 / value
    return first * (2.0 - value * first)


def kernel(
    dims,
    cj_ref,
    pj_ref,
    obs_ref,
    cnt_ref,
    back_ref,
    front_ref,
    damp_ref,
    cdamp_ref,
    rhs_ref,
    guess_ref,
    x_ref,
    r_ref,
    oh_lo,
    oh_hi,
    left,
    pieces,
    err,
    wts,
    table,
    next_out0,
    prev_out0,
    from_prev0,
    from_next0,
    next_out,
    prev_out,
    from_prev,
    from_next,
    red_out,
    red_in,
    ex_send,
    ex_recv,
    red_send,
    red_recv,
):
    nx, nz, ny, nc = dims
    total = nx * nz * ny * nc
    cams, slots = obs_ref.shape
    tiles = slots // 128
    me = lax.axis_index("seg")
    core = lax.rem(me, nc)
    y = lax.rem(me // nc, ny)
    z = lax.rem(me // (nc * ny), nz)
    x = me // (nc * ny * nz)

    def ident(px, pz, py, pc):
        return ((px * nz + pz) * ny + py) * nc + pc

    def plane(step):
        px = lax.rem(x + step // ny, nx)
        py = lax.rem(y + step % ny, ny)
        return ident(px, z, py, core)

    def column(step):
        pz = lax.rem(z + step // nc, nz)
        pc = lax.rem(core + step % nc, nc)
        return ident(x, pz, y, pc)

    plane_size, column_size = nx * ny, nz * nc
    plane_me, column_me = x * ny + y, z * nc + core

    def plane_slot(step):
        return lax.rem(x - step // ny + nx, nx) * ny + lax.rem(y - step % ny + ny, ny)

    def column_slot(step):
        return lax.rem(z - step // nc + nz, nz) * nc + lax.rem(core - step % nc + nc, nc)

    has_next, has_prev = me < total - 1, me > 0

    barrier = pltpu.get_barrier_semaphore()
    for step in range(1, plane_size):
        pl.semaphore_signal(barrier, inc=1, device_id=(plane(step),), device_id_type=MESH)
    for step in range(1, column_size):
        pl.semaphore_signal(barrier, inc=1, device_id=(column(step),), device_id_type=MESH)

    @pl.when(has_next)
    def _():
        pl.semaphore_signal(barrier, inc=1, device_id=(me + 1,), device_id_type=MESH)

    @pl.when(has_prev)
    def _():
        pl.semaphore_signal(barrier, inc=1, device_id=(me - 1,), device_id_type=MESH)

    @pl.when(jnp.logical_not(has_prev))
    def _():
        from_prev0[...] = jnp.zeros_like(from_prev0)
        from_prev[...] = jnp.zeros_like(from_prev)

    @pl.when(jnp.logical_not(has_next))
    def _():
        from_next0[...] = jnp.zeros_like(from_next0)
        from_next[...] = jnp.zeros_like(from_next)

    def border_copies(index, to_next, to_prev, came_prev, came_next):
        ahead = pltpu.make_async_remote_copy(
            src_ref=to_next,
            dst_ref=came_prev,
            send_sem=ex_send.at[index, 0],
            recv_sem=ex_recv.at[index, 0],
            device_id=(jnp.minimum(me + 1, total - 1),),
            device_id_type=MESH,
        )
        behind = pltpu.make_async_remote_copy(
            src_ref=to_prev,
            dst_ref=came_next,
            send_sem=ex_send.at[index, 1],
            recv_sem=ex_recv.at[index, 1],
            device_id=(jnp.maximum(me - 1, 0),),
            device_id_type=MESH,
        )
        return ahead, behind

    def border_start(copies):
        ahead, behind = copies

        @pl.when(has_next)
        def _():
            ahead.start()

        @pl.when(has_prev)
        def _():
            behind.start()

    def border_wait(copies):
        ahead, behind = copies

        @pl.when(has_prev)
        def _():
            ahead.wait_recv()
            behind.wait_send()

        @pl.when(has_next)
        def _():
            behind.wait_recv()
            ahead.wait_send()

    def group_copies(stage, size, mine, peer, slot):
        sends = []
        for step in range(1, size):
            sends.append(
                pltpu.make_async_remote_copy(
                    src_ref=red_out.at[stage],
                    dst_ref=red_in.at[stage, mine],
                    send_sem=red_send.at[stage, step - 1],
                    recv_sem=red_recv.at[stage, step - 1],
                    device_id=(peer(step),),
                    device_id_type=MESH,
                )
            )
        waits = []
        for step in range(1, size):
            waits.append(
                pltpu.make_async_remote_copy(
                    src_ref=red_out.at[stage],
                    dst_ref=red_in.at[stage, slot(step)],
                    send_sem=red_send.at[stage, step - 1],
                    recv_sem=red_recv.at[stage, step - 1],
                    device_id=(peer(step),),
                    device_id_type=MESH,
                )
            )
        return sends, waits

    def group_start(stage, value, size, mine, peer, slot):
        sends, waits = group_copies(stage, size, mine, peer, slot)
        red_out[stage] = value
        red_in[stage, mine] = value
        for copy in sends:
            copy.start()
        return sends, waits

    def group_finish(stage, copies, size):
        sends, waits = copies
        for copy in waits:
            copy.wait_recv()
        for copy in sends:
            copy.wait_send()
        result = red_in[stage, 0]
        for step in range(1, size):
            result = result + red_in[stage, step]
        return result

    plane_args = (plane_size, plane_me, plane, plane_slot)
    column_args = (column_size, column_me, column, column_slot)

    eye = lax.broadcasted_iota(jnp.int32, (cams, cams), 0) == lax.broadcasted_iota(
        jnp.int32, (cams, cams), 1
    )

    def stand(row):
        summed = jnp.sum(jnp.where(eye, spread(row, cams), 0.0), axis=1, keepdims=True)
        return jnp.broadcast_to(summed, (cams, 128))

    eye_wide = lax.broadcasted_iota(jnp.int32, (cams, 128), 0) == lax.broadcasted_iota(
        jnp.int32, (cams, 128), 1
    )

    def lie(block):
        return jnp.sum(jnp.where(eye_wide, block, 0.0), axis=0, keepdims=True)[:, :cams]

    def wide(block):
        return jnp.concatenate([block] * tiles, axis=1)

    def stack(block):
        return jnp.concatenate(
            [block[:, 128 * t : 128 * (t + 1)] for t in range(tiles)], axis=0
        )

    def narrow_sum(block):
        summed = jnp.sum(block, axis=1, keepdims=True)
        return jnp.broadcast_to(summed, (cams, 128))

    def inner(first, second):
        running = first[0] * second[0]
        for k in range(1, 9):
            running = running + first[k] * second[k]
        return jnp.sum(running, axis=0, keepdims=True)

    count = stand(cnt_ref[...].astype(F32))
    cam_damp = stand(cdamp_ref[...])
    guess = [stand(guess_ref[k : k + 1, :]) for k in range(9)]
    right = [stand(rhs_ref[k : k + 1, :]) for k in range(9)]
    position = lax.broadcasted_iota(jnp.int32, (cams, slots), 1).astype(F32)
    wts[...] = jnp.where(position < wide(count), 1.0, 0.0)

    lo_line = lax.broadcasted_iota(jnp.int32, (128, slots), 0).astype(F32).astype(BF16)
    hi_line = lax.broadcasted_iota(jnp.int32, (16, slots), 0).astype(F32).astype(BF16)
    one, none = jnp.ones((), BF16), jnp.zeros((), BF16)
    for c in range(cams):
        row = obs_ref[c : c + 1, :]
        low = (row & 127).astype(F32)
        high = (row >> 7).astype(F32)
        here = pl.ds(c * slots, slots)
        oh_lo[:, here] = jnp.where(spread(low, 128).astype(BF16) == lo_line, one, none)
        oh_hi[:, here] = jnp.where(spread(high, 16).astype(BF16) == hi_line, one, none)

    def scatter(groups):
        for c in range(cams):
            here = pl.ds(c * slots, slots)
            mask = oh_hi[:, here]
            for g in range(groups):
                row = spread(pieces[g, c : c + 1, :], 16).astype(BF16)
                left[16 * g : 16 * (g + 1), here] = row * mask
        return lax.dot_general(
            left[: 16 * groups, :],
            oh_lo[...],
            (((1,), (1,)), ((), ())),
            preferred_element_type=F32,
        )

    def cut(index, value):
        first = value.astype(BF16).astype(F32)
        pieces[2 * index] = first
        pieces[2 * index + 1] = value - first

    def joined(result, index):
        return result[32 * index : 32 * index + 16] + result[32 * index + 16 : 32 * index + 32]

    def project(vector):
        weights = wts[...]
        for row in range(2):
            running = cj_ref[9 * row].astype(F32) * wide(vector[0])
            for k in range(1, 9):
                running = running + cj_ref[9 * row + k].astype(F32) * wide(vector[k])
            err[row] = running * weights
        return err[0], err[1]

    def products(base, errors):
        for column_index in range(3):
            cut(
                base + column_index,
                errors[0] * pj_ref[column_index].astype(F32)
                + errors[1] * pj_ref[3 + column_index].astype(F32),
            )

    rows = [back_ref[:, 128 * t : 128 * (t + 1)] for t in range(3)]
    rows += [front_ref[:, 128 * t : 128 * (t + 1)] for t in range(3)]
    rows += [jnp.zeros((2, 128), jnp.int32)]
    listed = jnp.concatenate(rows, axis=0)
    list_lo, list_hi = listed & 127, listed >> 7
    flat = jnp.concatenate([back_ref[...], front_ref[...]], axis=1)
    width = flat.shape[1]
    flat_lo = spread((flat & 127).astype(F32), 128)
    flat_hi = spread((flat >> 7).astype(F32), 8)
    order = lax.broadcasted_iota(jnp.int32, (8, width), 1)
    hot_lo = jnp.where(
        flat_lo == lax.broadcasted_iota(jnp.int32, (128, width), 0).astype(F32), 1.0, 0.0
    ).astype(BF16)
    same_hi = flat_hi == lax.broadcasted_iota(jnp.int32, (8, width), 0).astype(F32)
    marks = jnp.concatenate(
        [
            jnp.where(same_hi, (order & 127).astype(F32), 0.0),
            jnp.where(same_hi, ((order >> 7) + 1).astype(F32), 0.0),
        ],
        axis=0,
    ).astype(BF16)
    places = lax.dot_general(
        marks, hot_lo, (((1,), (1,)), ((), ())), preferred_element_type=F32
    ).astype(jnp.int32)
    place_lo, place_hi = places[:8], places[8:16] - 1

    sub8 = lax.broadcasted_iota(jnp.int32, (8, 128), 0)
    back_rows = sub8 < 3

    def outgoing(sums, index, to_next, to_prev):
        own, outer = sums[:8], sums[8:16]
        picked = jnp.zeros((8, 128), F32)
        for h in range(8):
            found = lane_pick(spread(own[h : h + 1], 8), list_lo)
            picked = jnp.where(list_hi == h, found, picked)
        to_next[index] = jnp.where(back_rows, picked, outer)
        to_prev[index] = jnp.where(back_rows, outer, picked)

    def complete(sums, prev_block, next_block):
        own, outer = sums[:8], sums[8:16]
        mixed = jnp.where(back_rows, next_block, prev_block)
        added = jnp.zeros((8, 128), F32)
        for h in range(6):
            found = lane_pick(spread(mixed[h : h + 1], 8), place_lo)
            added = jnp.where(place_hi == h, found, added)
        return jnp.concatenate(
            [own + added, outer + jnp.where(back_rows, prev_block, next_block)], axis=0
        )

    obs_lo, obs_hi = stack(obs_ref[...] & 127), stack(obs_ref[...] >> 7)

    def finish(vector, errors, sums, inverse):
        points = [
            inverse[0] * sums[0] + inverse[1] * sums[1] + inverse[2] * sums[2],
            inverse[1] * sums[0] + inverse[3] * sums[1] + inverse[4] * sums[2],
            inverse[2] * sums[0] + inverse[4] * sums[1] + inverse[5] * sums[2],
        ]
        for j in range(3):
            table[j] = points[j]
        picked = []
        for j in range(3):
            found = jnp.zeros((cams * tiles, 128), F32)
            for h in range(14):
                row = spread(table[j, h : h + 1, :], cams * tiles)
                found = jnp.where(obs_hi == h, lane_pick(row, obs_lo), found)
            picked.append(
                jnp.concatenate(
                    [found[cams * t : cams * (t + 1)] for t in range(tiles)], axis=1
                )
            )
        weights = wts[...]
        adjusted = []
        for row in range(2):
            term = picked[0] * pj_ref[3 * row].astype(F32)
            term = term + picked[1] * pj_ref[3 * row + 1].astype(F32)
            term = term + picked[2] * pj_ref[3 * row + 2].astype(F32)
            adjusted.append(errors[row] - weights * term)
        image = []
        for k in range(9):
            both = (
                cj_ref[k].astype(F32) * adjusted[0] + cj_ref[9 + k].astype(F32) * adjusted[1]
            )
            image.append(cam_damp * vector[k] + narrow_sum(both))
        return image

    errors = project(guess)
    weights = wts[...]
    for i, (a, b) in enumerate(PAIRS):
        product = pj_ref[a].astype(F32) * pj_ref[b].astype(F32)
        product = product + pj_ref[3 + a].astype(F32) * pj_ref[3 + b].astype(F32)
        cut(i, product * weights)
    products(6, errors)
    result = scatter(18)
    sums = []
    damping = jnp.concatenate([damp_ref[...], jnp.zeros((8, 128), F32)], axis=0)
    for i in range(9):
        value = joined(result, i)
        if i < 6 and PAIRS[i][0] == PAIRS[i][1]:
            value = value + damping
        outgoing(value, i, next_out0, prev_out0)
        sums.append(value)
    pl.semaphore_wait(
        barrier,
        plane_size + column_size - 2 + has_next.astype(jnp.int32) + has_prev.astype(jnp.int32),
    )
    copies = border_copies(0, next_out0, prev_out0, from_prev0, from_next0)
    border_start(copies)
    precond = []
    for k in range(9):
        square = cj_ref[k].astype(F32) ** 2 + cj_ref[9 + k].astype(F32) ** 2
        precond.append(recip(cam_damp + narrow_sum(square * weights)))
    border_wait(copies)
    sums = [complete(sums[i], from_prev0[i], from_next0[i]) for i in range(9)]
    ent = sums[:6]
    cofactors = [
        ent[3] * ent[5] - ent[4] * ent[4],
        ent[2] * ent[4] - ent[1] * ent[5],
        ent[1] * ent[4] - ent[2] * ent[3],
        ent[0] * ent[5] - ent[2] * ent[2],
        ent[1] * ent[2] - ent[0] * ent[4],
        ent[0] * ent[3] - ent[1] * ent[1],
    ]
    determinant = ent[0] * cofactors[0] + ent[1] * cofactors[1] + ent[2] * cofactors[2]
    scale = recip(jnp.where(determinant > 0.0, determinant, 1.0))
    inverse = [member * scale for member in cofactors]
    image = finish(guess, errors, sums[6:], inverse)
    res0 = [right[k] - image[k] for k in range(9)]
    dir0 = [precond[k] * res0[k] for k in range(9)]

    def forward(vector, index):
        errors = project(vector)
        products(0, errors)
        result = scatter(6)
        sums = [joined(result, i) for i in range(3)]
        to_next, to_prev = next_out.at[index], prev_out.at[index]
        for i in range(3):
            outgoing(sums[i], i, to_next, to_prev)
        copies = border_copies(
            1 + index, to_next, to_prev, from_prev.at[index], from_next.at[index]
        )
        border_start(copies)
        return errors, sums, copies

    def backward(vector, index, errors, sums):
        sums = [complete(sums[i], from_prev[index, i], from_next[index, i]) for i in range(3)]
        return finish(vector, errors, sums, inverse)

    lane = lax.broadcasted_iota(jnp.int32, (1, 128), 1)

    def pack(first, second):
        return jnp.where(lane == 0, first, second)

    def unpack(row):
        first = jnp.sum(jnp.where(lane == 0, row, 0.0), axis=1, keepdims=True)
        second = jnp.sum(jnp.where(lane == 1, row, 0.0), axis=1, keepdims=True)
        return jnp.broadcast_to(first, (1, 128)), jnp.broadcast_to(second, (1, 128))

    errors, sums, copies = forward(dir0, 0)
    border_wait(copies)
    img0 = backward(dir0, 0, errors, sums)
    scaled = [precond[k] * img0[k] for k in range(9)]
    reducing = group_start(0, pack(inner(res0, dir0), inner(dir0, img0)), *plane_args)
    errors, sums, copies = forward(scaled, 1)
    value = group_finish(0, reducing, plane_size)
    reducing = group_start(1, value, *column_args)
    border_wait(copies)
    lift = backward(scaled, 1, errors, sums)
    inner0, curve0 = unpack(group_finish(1, reducing, column_size))
    step0 = inner0 * recip(curve0)
    res1 = [res0[k] - step0 * img0[k] for k in range(9)]
    dir1 = [dir0[k] - step0 * scaled[k] for k in range(9)]
    img1 = [img0[k] - step0 * lift[k] for k in range(9)]
    reducing = group_start(2, pack(inner(res1, dir1), inner(dir1, img1)), *plane_args)
    value = group_finish(2, reducing, plane_size)
    reducing = group_start(3, value, *column_args)
    inner1, curve1 = unpack(group_finish(3, reducing, column_size))
    ratio = inner1 * recip(inner0)
    step1 = inner1 * recip(curve1 - ratio * inner1 * recip(step0))
    for k in range(9):
        moved = guess[k] + step0 * dir0[k] + step1 * (dir1[k] + ratio * dir0[k])
        x_ref[k : k + 1, :] = lie(moved)
        left_over = res1[k] - step1 * (img1[k] + ratio * img0[k])
        r_ref[k : k + 1, :] = lie(left_over)


def local(dims, cam_jac, point_jac, obs_point, obs_count, back_list, front_list, point_damp,
          cam_damp, right_side, start_guess):
    cams, slots = obs_point.shape
    entries = cams * slots
    nx, nz, ny, nc = dims
    group = max(nx * ny, nz * nc)
    vmem = pl.BlockSpec(memory_space=pltpu.VMEM)
    shape = jax.ShapeDtypeStruct(right_side.shape, F32)
    return pl.pallas_call(
        functools.partial(kernel, dims),
        out_shape=(shape, shape),
        in_specs=[vmem] * 10,
        out_specs=(vmem, vmem),
        scratch_shapes=[
            pltpu.VMEM((128, entries), BF16),
            pltpu.VMEM((16, entries), BF16),
            pltpu.VMEM((288, entries), BF16),
            pltpu.VMEM((18, cams, slots), F32),
            pltpu.VMEM((2, cams, slots), F32),
            pltpu.VMEM((cams, slots), F32),
            pltpu.VMEM((3, 16, 128), F32),
            pltpu.VMEM((9, 8, 128), F32),
            pltpu.VMEM((9, 8, 128), F32),
            pltpu.VMEM((9, 8, 128), F32),
            pltpu.VMEM((9, 8, 128), F32),
            pltpu.VMEM((2, 3, 8, 128), F32),
            pltpu.VMEM((2, 3, 8, 128), F32),
            pltpu.VMEM((2, 3, 8, 128), F32),
            pltpu.VMEM((2, 3, 8, 128), F32),
            pltpu.VMEM((4, 1, 128), F32),
            pltpu.VMEM((4, group, 1, 128), F32),
            pltpu.SemaphoreType.DMA((3, 2)),
            pltpu.SemaphoreType.DMA((3, 2)),
            pltpu.SemaphoreType.DMA((4, group - 1)),
            pltpu.SemaphoreType.DMA((4, group - 1)),
        ],
        compiler_params=pltpu.CompilerParams(
            collective_id=0, has_side_effects=True, vmem_limit_bytes=48 * 1024 * 1024
        ),
    )(
        cam_jac,
        point_jac,
        obs_point,
        obs_count.reshape(1, cams),
        back_list,
        front_list,
        point_damp.reshape(8, 128),
        cam_damp.reshape(1, cams),
        right_side,
        start_guess,
    )


def solution(mesh):
    seg = "seg"
    return jax.shard_map(
        functools.partial(local, DIMS),
        mesh=mesh,
        in_specs=(
            P(None, seg, None),
            P(None, seg, None),
            P(seg, None),
            P(seg),
            P(seg, None),
            P(seg, None),
            P(seg),
            P(seg),
            P(None, seg),
            P(None, seg),
        ),
        out_specs=(P(None, seg), P(None, seg)),
        check_vma=False,
    )
```

time: 973 us -> 51.3 us (0.05)
  other arithmetic: 687 us -> 0 us
  local copies, waits for them, and re-layouts: 132 us -> 7.87 us
  blocking collectives: 86.1 us -> 0 us
  Pallas kernels: 0 us -> 42.4 us
  starting transfers between devices: 35.7 us -> 0 us
  waiting for transfers between devices: 17.3 us -> 0 us
    scatter-add x23 -> x0, other arithmetic: 679 us -> none  [the longest x9 394 us: operator(): jax.ops.segment_sum(product.reshape(-1), owners, num_segments=extended)]
    gather x19 -> x0, local copies, waits for them, and re-layouts: 92.8 us -> none  [the longest x3 83.1 us: operator(): picked = values[:, owners].reshape(3, cameras, slot_total)]
    psum x8 -> x0, blocking collectives: 86.1 us -> none  [by_axis(): shard = lax.psum(shard, axis)]
    pallas_call x0 -> x1, Pallas kernels: none -> 42.4 us  [local(): pl.pallas_call(functools.partial(kernel, dims), out_shape=(shape, shape),...]
    ppermute x8 -> x0, starting transfers between devices: 35.7 us -> none  [the longest x4 27.6 us: padded(): lax.ppermute(lax.slice_in_dim(block, 0, width, axis=dim), axis, backward)]
    slice x17 -> x0, local copies, waits for them, and re-layouts: 31.8 us -> none  [the longest x3 30.5 us: operator(): picked[2] * point_jac[3 * row_index + 2].astype(jnp.float32)]
    ppermute x8 -> x0, waiting for transfers between devices: 17.3 us -> none  [the longest x4 17.3 us: padded(): lax.ppermute(lax.slice_in_dim(block, block.shape[dim] - width, None, axis...]
  transfers between devices with their start and end apart: 8 -> 0, of which waited for: 3 -> 0; matrix products, arithmetic and copies ran while one was open for 16% -> 0% of each run, Pallas kernels for 0% -> 0%
where the time goes in v1:
time: 51.3 us; the launch traced here: 51 us
  Pallas kernels  42.4 us (83%)
  local copies, waits for them, and re-layouts  7.87 us (15%)
  between operations  0.67 us (1%)
    pallas_call x1, Pallas kernels, local(): pl.pallas_call(functools.partial(kernel, dims), out_shape=(shape, shape),...  42.4 us
    unnamed x22, local copies, waits for them, and re-layouts  7.87 us

profile of v1, /device:TPU:1, one launch (start us, length us, event | category | flops | bytes accessed | tf_op | source)
XLA Modules:
  0.0 51.0 jit_solution(266834797907618061)
XLA Ops:
  0.6 0.0 copy-start.5
  0.6 0.0 copy-start.6
  0.7 0.7 %copy-done.5 = f32[1024]{0:T(1024)S(1)} copy-done((f32[1024]{0:T(1024)S(1)}, f32[1024]{0:T(1024)}, u32[]{:S(2)}) %copy-start.5) | copy-done | bytes 4120
  1.3 0.0 copy-done.6
  1.3 0.0 copy-start
  1.3 1.0 %copy-done = bf16[18,16,512]{2,1,0:T(8,128)(2,1)S(1)} copy-done((bf16[18,16,512]{2,1,0:T(8,128)(2,1)S(1)}, bf16[18,16,512]{2,1,0:T(8,128)(2,1)}, u32[]{:S(2)}) %copy-start) | copy-done | bytes 294936
  2.3 0.0 copy-start.1
  2.3 0.9 %copy-done.1 = bf16[6,16,512]{2,1,0:T(8,128)(2,1)S(1)} copy-done((bf16[6,16,512]{2,1,0:T(8,128)(2,1)S(1)}, bf16[6,16,512]{2,1,0:T(8,128)(2,1)}, u32[]{:S(2)}) %copy-start.1) | copy-done | bytes 98328
  3.2 0.0 copy-start.2
  3.2 0.8 %copy-done.2 = s32[16,512]{1,0:T(8,128)S(1)} copy-done((s32[16,512]{1,0:T(8,128)S(1)}, s32[16,512]{1,0:T(8,128)}, u32[]{:S(2)}) %copy-start.2) | copy-done | bytes 32792
  3.9 0.0 copy-start.3
  3.9 0.7 %copy-done.3 = f32[9,16]{1,0:T(8,128)S(1)} copy-done((f32[9,16]{1,0:T(8,128)S(1)}, f32[9,16]{1,0:T(8,128)}, u32[]{:S(2)}) %copy-start.3) | copy-done | bytes 600
  4.6 0.0 copy-start.4
  4.6 0.7 %copy-done.4 = f32[9,16]{1,0:T(8,128)S(1)} copy-done((f32[9,16]{1,0:T(8,128)S(1)}, f32[9,16]{1,0:T(8,128)}, u32[]{:S(2)}) %copy-start.4) | copy-done | bytes 600
  5.3 0.0 copy-start.7
  5.3 0.7 %copy-done.7 = s32[1,384]{1,0:T(1,128)S(1)} copy-done((s32[1,384]{1,0:T(1,128)S(1)}, s32[1,384]{1,0:T(1,128)}, u32[]{:S(2)}) %copy-start.7) | copy-done | bytes 1560
  6.0 0.0 copy-start.8
  6.0 0.7 %copy-done.8 = s32[16]{0:T(128)S(1)} copy-done((s32[16]{0:T(128)S(1)}, s32[16]{0:T(128)}, u32[]{:S(2)}) %copy-start.8) | copy-done | bytes 88
  6.7 0.0 copy-start.9
  6.7 0.7 %copy-done.9 = f32[16]{0:T(128)S(1)} copy-done((f32[16]{0:T(128)S(1)}, f32[16]{0:T(128)}, u32[]{:S(2)}) %copy-start.9) | copy-done | bytes 88
  7.3 42.4 %shard_map.113 = (f32[9,16]{1,0:T(8,128)S(1)}, f32[9,16]{1,0:T(8,128)S(1)}) custom-call(bf16[18,16,512]{2,1,0:T(8,128)(2,1)S(1)} %copy-done, bf16[6,16,512]{2,1,0:T(8,128)(2,1)S(1)} %copy-done.1, s32[16,512]{1,0:T(8,128)S(1)} %copy-done.2, s32[1,16]{1,0:T(1,128)S(1)} %bitcast.4, s32[1,384]{1,0:T(1,128)S(1)} %copy-done.6, s32[1,384]{1,0:T(1,128)S(1)} %copy-done.7, ...), custom_call_target="tpu_custom_call" | custom-call | tf_op jit(solution)/shard_map/pallas_call | solution.py:499
  49.8 0.6 %copy.14 = f32[9,16]{1,0:T(8,128)} copy(f32[9,16]{1,0:T(8,128)S(1)} %get-tuple-element.4) | data formatting | bytes 1152
  50.4 0.6 %copy.15 = f32[9,16]{1,0:T(8,128)} copy(f32[9,16]{1,0:T(8,128)S(1)} %get-tuple-element.5) | data formatting | bytes 1152
Async XLA Ops:
  0.6 0.7 %copy-start.5 = (f32[1024]{0:T(1024)S(1)}, f32[1024]{0:T(1024)}, u32[]{:S(2)}) copy-start(f32[1024]{0:T(1024)} %param.16) | copy-start | bytes 12292
  0.6 0.7 %copy-start.6 = (s32[1,384]{1,0:T(1,128)S(1)}, s32[1,384]{1,0:T(1,128)}, u32[]{:S(2)}) copy-start(s32[1,384]{1,0:T(1,128)} %back_ref.1) | copy-start | bytes 4612
  1.3 1.0 %copy-start = (bf16[18,16,512]{2,1,0:T(8,128)(2,1)S(1)}, bf16[18,16,512]{2,1,0:T(8,128)(2,1)}, u32[]{:S(2)}) copy-start(bf16[18,16,512]{2,1,0:T(8,128)(2,1)} %cj_ref.1) | copy-start | bytes 884740
  2.3 0.9 %copy-start.1 = (bf16[6,16,512]{2,1,0:T(8,128)(2,1)S(1)}, bf16[6,16,512]{2,1,0:T(8,128)(2,1)}, u32[]{:S(2)}) copy-start(bf16[6,16,512]{2,1,0:T(8,128)(2,1)} %pj_ref.1) | copy-start | bytes 294916
  3.2 0.8 %copy-start.2 = (s32[16,512]{1,0:T(8,128)S(1)}, s32[16,512]{1,0:T(8,128)}, u32[]{:S(2)}) copy-start(s32[16,512]{1,0:T(8,128)} %obs_ref.1) | copy-start | bytes 98308
  3.9 0.7 %copy-start.3 = (f32[9,16]{1,0:T(8,128)S(1)}, f32[9,16]{1,0:T(8,128)}, u32[]{:S(2)}) copy-start(f32[9,16]{1,0:T(8,128)} %rhs_ref.1) | copy-start | bytes 1732
  4.6 0.7 %copy-start.4 = (f32[9,16]{1,0:T(8,128)S(1)}, f32[9,16]{1,0:T(8,128)}, u32[]{:S(2)}) copy-start(f32[9,16]{1,0:T(8,128)} %guess_ref.1) | copy-start | bytes 1732
  5.3 0.7 %copy-start.7 = (s32[1,384]{1,0:T(1,128)S(1)}, s32[1,384]{1,0:T(1,128)}, u32[]{:S(2)}) copy-start(s32[1,384]{1,0:T(1,128)} %front_ref.1) | copy-start | bytes 4612
  6.0 0.7 %copy-start.8 = (s32[16]{0:T(128)S(1)}, s32[16]{0:T(128)}, u32[]{:S(2)}) copy-start(s32[16]{0:T(128)} %param.13) | copy-start | bytes 196
  6.7 0.7 %copy-start.9 = (f32[16]{0:T(128)S(1)}, f32[16]{0:T(128)}, u32[]{:S(2)}) copy-start(f32[16]{0:T(128)} %param.17) | copy-start | bytes 196

commit v2 on v1

--- a/solution.py
+++ b/solution.py
@@ -8,6 +8,7 @@
 from jax.sharding import PartitionSpec as P
 
 DIMS = (4, 8, 4, 2)
+HUB = 1
 PAIRS = ((0, 0), (0, 1), (0, 2), (1, 1), (1, 2), (2, 2))
 F32 = jnp.float32
 BF16 = jnp.bfloat16
@@ -29,6 +30,17 @@
 
 def kernel(
     dims,
+    cj_hbm,
+    pj_hbm,
+    obs_hbm,
+    cnt_hbm,
+    back_hbm,
+    front_hbm,
+    damp_hbm,
+    cdamp_hbm,
+    rhs_hbm,
+    guess_hbm,
+    out_ref,
     cj_ref,
     pj_ref,
     obs_ref,
@@ -39,8 +51,7 @@
     cdamp_ref,
     rhs_ref,
     guess_ref,
-    x_ref,
-    r_ref,
+    load_sem,
     oh_lo,
     oh_hi,
     left,
@@ -56,15 +67,37 @@
     prev_out,
     from_prev,
     from_next,
-    red_out,
-    red_in,
+    first_out,
+    first_in,
+    second_out,
+    second_in,
     ex_send,
     ex_recv,
-    red_send,
-    red_recv,
+    first_send,
+    first_recv,
+    second_send,
+    second_recv,
 ):
     nx, nz, ny, nc = dims
     total = nx * nz * ny * nc
+    arrivals = [
+        (obs_hbm, obs_ref),
+        (cnt_hbm, cnt_ref),
+        (guess_hbm, guess_ref),
+        (back_hbm, back_ref),
+        (front_hbm, front_ref),
+        (pj_hbm, pj_ref),
+        (cj_hbm, cj_ref),
+        (damp_hbm, damp_ref),
+        (cdamp_hbm, cdamp_ref),
+        (rhs_hbm, rhs_ref),
+    ]
+    loads = [
+        pltpu.make_async_copy(source, target, load_sem.at[i])
+        for i, (source, target) in enumerate(arrivals)
+    ]
+    for load in loads:
+        load.start()
     cams, slots = obs_ref.shape
     tiles = slots // 128
     me = lax.axis_index("seg")
@@ -76,32 +109,38 @@
     def ident(px, pz, py, pc):
         return ((px * nz + pz) * ny + py) * nc + pc
 
-    def plane(step):
-        px = lax.rem(x + step // ny, nx)
-        py = lax.rem(y + step % ny, ny)
-        return ident(px, z, py, core)
-
-    def column(step):
-        pz = lax.rem(z + step // nc, nz)
-        pc = lax.rem(core + step % nc, nc)
-        return ident(x, pz, y, pc)
-
-    plane_size, column_size = nx * ny, nz * nc
-    plane_me, column_me = x * ny + y, z * nc + core
-
-    def plane_slot(step):
-        return lax.rem(x - step // ny + nx, nx) * ny + lax.rem(y - step % ny + ny, ny)
-
-    def column_slot(step):
-        return lax.rem(z - step // nc + nz, nz) * nc + lax.rem(core - step % nc + nc, nc)
+    plane_size = nx * ny
+    hub = core == HUB
+
+    def plane_at(step, sign):
+        px = lax.rem(x + (step // ny if sign > 0 else nx - step // ny), nx)
+        py = lax.rem(y + (step % ny if sign > 0 else ny - step % ny), ny)
+        return px, py
+
+    def height_at(step, sign):
+        return lax.rem(z + (step if sign > 0 else nz - step), nz)
 
     has_next, has_prev = me < total - 1, me > 0
 
     barrier = pltpu.get_barrier_semaphore()
-    for step in range(1, plane_size):
-        pl.semaphore_signal(barrier, inc=1, device_id=(plane(step),), device_id_type=MESH)
-    for step in range(1, column_size):
-        pl.semaphore_signal(barrier, inc=1, device_id=(column(step),), device_id_type=MESH)
+
+    def greet(device):
+        pl.semaphore_signal(barrier, inc=1, device_id=(device,), device_id_type=MESH)
+
+    @pl.when(hub)
+    def _():
+        for step in range(plane_size):
+            px, py = plane_at(step, -1)
+            for pc in range(nc):
+                if step or pc != HUB:
+                    greet(ident(px, z, py, pc))
+
+    for step in range(1, nz):
+        greet(ident(x, height_at(step, -1), y, HUB))
+
+    @pl.when(jnp.logical_not(hub))
+    def _():
+        greet(ident(x, z, y, HUB))
 
     @pl.when(has_next)
     def _():
@@ -164,54 +203,94 @@
             behind.wait_recv()
             ahead.wait_send()
 
-    def group_copies(stage, size, mine, peer, slot):
-        sends = []
-        for step in range(1, size):
-            sends.append(
-                pltpu.make_async_remote_copy(
-                    src_ref=red_out.at[stage],
-                    dst_ref=red_in.at[stage, mine],
-                    send_sem=red_send.at[stage, step - 1],
-                    recv_sem=red_recv.at[stage, step - 1],
-                    device_id=(peer(step),),
-                    device_id_type=MESH,
-                )
-            )
-        waits = []
-        for step in range(1, size):
-            waits.append(
-                pltpu.make_async_remote_copy(
-                    src_ref=red_out.at[stage],
-                    dst_ref=red_in.at[stage, slot(step)],
-                    send_sem=red_send.at[stage, step - 1],
-                    recv_sem=red_recv.at[stage, step - 1],
-                    device_id=(peer(step),),
-                    device_id_type=MESH,
-                )
-            )
-        return sends, waits
-
-    def group_start(stage, value, size, mine, peer, slot):
-        sends, waits = group_copies(stage, size, mine, peer, slot)
-        red_out[stage] = value
-        red_in[stage, mine] = value
-        for copy in sends:
-            copy.start()
-        return sends, waits
-
-    def group_finish(stage, copies, size):
-        sends, waits = copies
-        for copy in waits:
-            copy.wait_recv()
-        for copy in sends:
-            copy.wait_send()
-        result = red_in[stage, 0]
-        for step in range(1, size):
-            result = result + red_in[stage, step]
-        return result
-
-    plane_args = (plane_size, plane_me, plane, plane_slot)
-    column_args = (column_size, column_me, column, column_slot)
+    plane_me = (x * ny + y) * nc + core
+
+    def first_copy(step, sender_core, slot):
+        px, py = plane_at(step, 1)
+        return pltpu.make_async_remote_copy(
+            src_ref=first_out,
+            dst_ref=first_in.at[slot],
+            send_sem=first_send.at[step],
+            recv_sem=first_recv.at[step * nc + sender_core],
+            device_id=(ident(px, z, py, HUB),),
+            device_id_type=MESH,
+        )
+
+    def second_copy(step, pc, slot):
+        return pltpu.make_async_remote_copy(
+            src_ref=second_out,
+            dst_ref=second_in.at[slot],
+            send_sem=second_send.at[step * nc + pc],
+            recv_sem=second_recv.at[step],
+            device_id=(ident(x, height_at(step, 1), y, pc),),
+            device_id_type=MESH,
+        )
+
+    far_first = sorted(
+        range(1, plane_size),
+        key=lambda step: -(
+            min(step // ny, nx - step // ny) + min(step % ny, ny - step % ny)
+        ),
+    )
+    high_first = sorted(range(1, nz), key=lambda step: -min(step, nz - step))
+
+    def reduce_start(value):
+        first_out[...] = value
+        for step in far_first:
+            first_copy(step, core, plane_me).start()
+
+        @pl.when(hub)
+        def _():
+            first_in[plane_me] = value
+
+        @pl.when(jnp.logical_not(hub))
+        def _():
+            first_copy(0, core, plane_me).start()
+
+    def reduce_finish():
+        @pl.when(hub)
+        def _():
+            for step in range(plane_size):
+                px, py = plane_at(step, -1)
+                for pc in range(nc):
+                    if step or pc != HUB:
+                        first_copy(step, pc, (px * ny + py) * nc + pc).wait_recv()
+            value = first_in[0]
+            for slot in range(1, plane_size * nc):
+                value = value + first_in[slot]
+            second_out[...] = value
+            second_in[z] = value
+            for step in high_first:
+                for pc in range(nc):
+                    second_copy(step, pc, z).start()
+            for pc in range(nc):
+                if pc != HUB:
+                    second_copy(0, pc, z).start()
+
+        for step in far_first:
+            first_copy(step, core, plane_me).wait_send()
+
+        @pl.when(jnp.logical_not(hub))
+        def _():
+            first_copy(0, core, plane_me).wait_send()
+            second_copy(0, core, z).wait_recv()
+
+        for step in range(1, nz):
+            second_copy(step, core, height_at(step, -1)).wait_recv()
+
+        @pl.when(hub)
+        def _():
+            for step in high_first:
+                for pc in range(nc):
+                    second_copy(step, pc, z).wait_send()
+            for pc in range(nc):
+                if pc != HUB:
+                    second_copy(0, pc, z).wait_send()
+
+        value = second_in[0]
+        for slot in range(1, nz):
+            value = value + second_in[slot]
+        return value
 
     eye = lax.broadcasted_iota(jnp.int32, (cams, cams), 0) == lax.broadcasted_iota(
         jnp.int32, (cams, cams), 1
@@ -246,10 +325,10 @@
             running = running + first[k] * second[k]
         return jnp.sum(running, axis=0, keepdims=True)
 
+    for load in loads[:5]:
+        load.wait()
     count = stand(cnt_ref[...].astype(F32))
-    cam_damp = stand(cdamp_ref[...])
     guess = [stand(guess_ref[k : k + 1, :]) for k in range(9)]
-    right = [stand(rhs_ref[k : k + 1, :]) for k in range(9)]
     position = lax.broadcasted_iota(jnp.int32, (cams, slots), 1).astype(F32)
     wts[...] = jnp.where(position < wide(count), 1.0, 0.0)
 
@@ -354,12 +433,14 @@
 
     obs_lo, obs_hi = stack(obs_ref[...] & 127), stack(obs_ref[...] >> 7)
 
-    def finish(vector, errors, sums, inverse):
-        points = [
+    def solve(sums, inverse):
+        return [
             inverse[0] * sums[0] + inverse[1] * sums[1] + inverse[2] * sums[2],
             inverse[1] * sums[0] + inverse[3] * sums[1] + inverse[4] * sums[2],
             inverse[2] * sums[0] + inverse[4] * sums[1] + inverse[5] * sums[2],
         ]
+
+    def finish(vector, errors, points):
         for j in range(3):
             table[j] = points[j]
         picked = []
@@ -388,6 +469,11 @@
             image.append(cam_damp * vector[k] + narrow_sum(both))
         return image
 
+    for load in loads[5:]:
+        load.wait()
+    cam_damp = stand(cdamp_ref[...])
+    right = [stand(rhs_ref[k : k + 1, :]) for k in range(9)]
+
     errors = project(guess)
     weights = wts[...]
     for i, (a, b) in enumerate(PAIRS):
@@ -406,7 +492,11 @@
         sums.append(value)
     pl.semaphore_wait(
         barrier,
-        plane_size + column_size - 2 + has_next.astype(jnp.int32) + has_prev.astype(jnp.int32),
+        plane_size
+        - hub.astype(jnp.int32)
+        + hub.astype(jnp.int32) * (nz * nc - 1)
+        + has_next.astype(jnp.int32)
+        + has_prev.astype(jnp.int32),
     )
     copies = border_copies(0, next_out0, prev_out0, from_prev0, from_next0)
     border_start(copies)
@@ -428,7 +518,7 @@
     determinant = ent[0] * cofactors[0] + ent[1] * cofactors[1] + ent[2] * cofactors[2]
     scale = recip(jnp.where(determinant > 0.0, determinant, 1.0))
     inverse = [member * scale for member in cofactors]
-    image = finish(guess, errors, sums[6:], inverse)
+    image = finish(guess, errors, solve(sums[6:], inverse))
     res0 = [right[k] - image[k] for k in range(9)]
     dir0 = [precond[k] * res0[k] for k in range(9)]
 
@@ -446,46 +536,61 @@
         border_start(copies)
         return errors, sums, copies
 
-    def backward(vector, index, errors, sums):
-        sums = [complete(sums[i], from_prev[index, i], from_next[index, i]) for i in range(3)]
-        return finish(vector, errors, sums, inverse)
+    def arrived(index, sums):
+        return [complete(sums[i], from_prev[index, i], from_next[index, i]) for i in range(3)]
 
     lane = lax.broadcasted_iota(jnp.int32, (1, 128), 1)
-
-    def pack(first, second):
-        return jnp.where(lane == 0, first, second)
-
-    def unpack(row):
-        first = jnp.sum(jnp.where(lane == 0, row, 0.0), axis=1, keepdims=True)
-        second = jnp.sum(jnp.where(lane == 1, row, 0.0), axis=1, keepdims=True)
-        return jnp.broadcast_to(first, (1, 128)), jnp.broadcast_to(second, (1, 128))
 
     errors, sums, copies = forward(dir0, 0)
     border_wait(copies)
-    img0 = backward(dir0, 0, errors, sums)
-    scaled = [precond[k] * img0[k] for k in range(9)]
-    reducing = group_start(0, pack(inner(res0, dir0), inner(dir0, img0)), *plane_args)
-    errors, sums, copies = forward(scaled, 1)
-    value = group_finish(0, reducing, plane_size)
-    reducing = group_start(1, value, *column_args)
+    sums = arrived(0, sums)
+    img0 = finish(dir0, errors, solve(sums, inverse))
+    res_t = [res0[k] - img0[k] for k in range(9)]
+    dir_t = [precond[k] * res_t[k] for k in range(9)]
+    errors, sums, copies = forward(dir_t, 1)
+    scalars = [
+        inner(res0, dir0),
+        inner(dir0, img0),
+        inner(res_t, dir0),
+        inner(img0, dir_t),
+        inner(res_t, dir_t),
+    ]
+    row = jnp.zeros((1, 128), F32)
+    for i, scalar in enumerate(scalars):
+        row = jnp.where(lane == i, scalar, row)
+    damped = jnp.sum(cam_damp * sum(entry * entry for entry in dir_t), axis=0, keepdims=True)
+    squares = errors[0] * errors[0] + errors[1] * errors[1]
+    squares = jnp.sum(squares, axis=0, keepdims=True)
+    squares = sum(squares[:, 128 * t : 128 * (t + 1)] for t in range(tiles))
     border_wait(copies)
-    lift = backward(scaled, 1, errors, sums)
-    inner0, curve0 = unpack(group_finish(1, reducing, column_size))
-    step0 = inner0 * recip(curve0)
-    res1 = [res0[k] - step0 * img0[k] for k in range(9)]
-    dir1 = [dir0[k] - step0 * scaled[k] for k in range(9)]
-    img1 = [img0[k] - step0 * lift[k] for k in range(9)]
-    reducing = group_start(2, pack(inner(res1, dir1), inner(dir1, img1)), *plane_args)
-    value = group_finish(2, reducing, plane_size)
-    reducing = group_start(3, value, *column_args)
-    inner1, curve1 = unpack(group_finish(3, reducing, column_size))
+    sums = arrived(1, sums)
+    points = solve(sums, inverse)
+    energy = sum(sums[j][:8] * points[j][:8] for j in range(3))
+    squares = squares - jnp.sum(energy, axis=0, keepdims=True)
+    curve_t = damped + jnp.sum(squares, axis=1, keepdims=True)
+    reduce_start(jnp.where(lane == len(scalars), curve_t, row))
+    img_t = finish(dir_t, errors, points)
+    row = reduce_finish()
+
+    def at(index):
+        picked = jnp.sum(jnp.where(lane == index, row, 0.0), axis=1, keepdims=True)
+        return jnp.broadcast_to(picked, (1, 128))
+
+    inner0, curve0, mixed_t, cross_t, inner_t, curve_t = [at(i) for i in range(6)]
+    shift = mixed_t * recip(curve0)
+    step0 = 1.0 + shift
+    inner1 = inner_t - 2.0 * shift * cross_t + shift * shift * (curve0 - cross_t)
+    curve1 = step0 * step0 * curve_t - 2.0 * shift * step0 * cross_t + shift * shift * curve0
     ratio = inner1 * recip(inner0)
     step1 = inner1 * recip(curve1 - ratio * inner1 * recip(step0))
+    dir1 = [step0 * dir_t[k] - shift * dir0[k] for k in range(9)]
+    res1 = [res_t[k] - shift * img0[k] for k in range(9)]
+    img1 = [step0 * img_t[k] - shift * img0[k] for k in range(9)]
     for k in range(9):
         moved = guess[k] + step0 * dir0[k] + step1 * (dir1[k] + ratio * dir0[k])
-        x_ref[k : k + 1, :] = lie(moved)
+        out_ref[0, k : k + 1, :] = lie(moved)
         left_over = res1[k] - step1 * (img1[k] + ratio * img0[k])
-        r_ref[k : k + 1, :] = lie(left_over)
+        out_ref[1, k : k + 1, :] = lie(left_over)
 
 
 def local(dims, cam_jac, point_jac, obs_point, obs_count, back_list, front_list, point_damp,
@@ -493,15 +598,29 @@
     cams, slots = obs_point.shape
     entries = cams * slots
     nx, nz, ny, nc = dims
-    group = max(nx * ny, nz * nc)
+    arrays = (
+        cam_jac,
+        point_jac,
+        obs_point,
+        obs_count.reshape(1, cams),
+        back_list,
+        front_list,
+        point_damp.reshape(8, 128),
+        cam_damp.reshape(1, cams),
+        right_side,
+        start_guess,
+    )
+    arrays = tuple(pltpu.with_memory_space_constraint(array, pltpu.HBM) for array in arrays)
     vmem = pl.BlockSpec(memory_space=pltpu.VMEM)
-    shape = jax.ShapeDtypeStruct(right_side.shape, F32)
-    return pl.pallas_call(
+    shape = jax.ShapeDtypeStruct((2, *right_side.shape), F32)
+    both = pl.pallas_call(
         functools.partial(kernel, dims),
-        out_shape=(shape, shape),
-        in_specs=[vmem] * 10,
-        out_specs=(vmem, vmem),
+        out_shape=shape,
+        in_specs=[pl.BlockSpec(memory_space=pltpu.HBM)] * len(arrays),
+        out_specs=vmem,
         scratch_shapes=[
+            *[pltpu.VMEM(array.shape, array.dtype) for array in arrays],
+            pltpu.SemaphoreType.DMA((len(arrays),)),
             pltpu.VMEM((128, entries), BF16),
             pltpu.VMEM((16, entries), BF16),
             pltpu.VMEM((288, entries), BF16),
@@ -517,28 +636,22 @@
             pltpu.VMEM((2, 3, 8, 128), F32),
             pltpu.VMEM((2, 3, 8, 128), F32),
             pltpu.VMEM((2, 3, 8, 128), F32),
-            pltpu.VMEM((4, 1, 128), F32),
-            pltpu.VMEM((4, group, 1, 128), F32),
+            pltpu.VMEM((1, 128), F32),
+            pltpu.VMEM((nx * ny * nc, 1, 128), F32),
+            pltpu.VMEM((1, 128), F32),
+            pltpu.VMEM((nz, 1, 128), F32),
             pltpu.SemaphoreType.DMA((3, 2)),
             pltpu.SemaphoreType.DMA((3, 2)),
-            pltpu.SemaphoreType.DMA((4, group - 1)),
-            pltpu.SemaphoreType.DMA((4, group - 1)),
+            pltpu.SemaphoreType.DMA((nx * ny,)),
+            pltpu.SemaphoreType.DMA((nx * ny * nc,)),
+            pltpu.SemaphoreType.DMA((nz * nc,)),
+            pltpu.SemaphoreType.DMA((nz,)),
         ],
         compiler_params=pltpu.CompilerParams(
             collective_id=0, has_side_effects=True, vmem_limit_bytes=48 * 1024 * 1024
         ),
-    )(
-        cam_jac,
-        point_jac,
-        obs_point,
-        obs_count.reshape(1, cams),
-        back_list,
-        front_list,
-        point_damp.reshape(8, 128),
-        cam_damp.reshape(1, cams),
-        right_side,
-        start_guess,
-    )
+    )(*arrays)
+    return both[0], both[1]
 
 
 def solution(mesh):

time: 51.3 us -> 38.3 us (0.75)
  local copies, waits for them, and re-layouts: 7.87 us -> 0.61 us
  Pallas kernels: 42.4 us -> 37 us
    unnamed x22 -> x0, local copies, waits for them, and re-layouts: 7.87 us -> none
    pallas_call x1, Pallas kernels: 42.4 us -> 37 us  [local(): pl.pallas_call(functools.partial(kernel, dims), out_shape=shape, in_specs...]
    squeeze x0 -> x1, local copies, waits for them, and re-layouts: none -> 0.61 us  [local(): return (both[0], both[1])]
where the time goes in v2:
time: 38.3 us; the launch traced here: 38.2 us
  Pallas kernels  37 us (97%)
  between operations  0.64 us (2%)
  local copies, waits for them, and re-layouts  0.61 us (2%)
    pallas_call x1, Pallas kernels, local(): pl.pallas_call(functools.partial(kernel, dims), out_shape=shape, in_specs...  37 us

profile of v2, /device:TPU:1, one launch (start us, length us, event | category | flops | bytes accessed | tf_op | source)
XLA Modules:
  0.0 38.2 jit_solution(3935936436977114216)
XLA Ops:
  0.6 37.0 %shard_map.113 = f32[2,9,16]{2,1,0:T(8,128)S(1)} custom-call(bf16[18,16,512]{2,1,0:T(8,128)(2,1)} %cj_hbm.1, bf16[6,16,512]{2,1,0:T(8,128)(2,1)} %pj_hbm.1, s32[16,512]{1,0:T(8,128)} %obs_hbm.1, s32[1,16]{1,0:T(1,128)} %bitcast.8, s32[1,384]{1,0:T(1,128)} %back_hbm.1, s32[1,384]{1,0:T(1,128)} %front_hbm.1, f32[8,128]{1,0:T(8,128)} %bitcast.7, ...), custom_call_target="tpu_custom_call" | custom-call | tf_op jit(solution)/shard_map/pallas_call | solution.py:616
  37.6 0.6 %slice_bitcast_fusion = (f32[9,16]{1,0:T(8,128)}, f32[9,16]{1,0:T(8,128)}) fusion(f32[2,9,16]{2,1,0:T(8,128)S(1)} %shard_map.113), kind=kLoop, calls=%fused_computation | loop fusion | bytes 2304 | tf_op jit(solution)/shard_map/squeeze | solution.py:654

commit v3 on v2

--- a/solution.py
+++ b/solution.py
@@ -12,6 +12,7 @@
 PAIRS = ((0, 0), (0, 1), (0, 2), (1, 1), (1, 2), (2, 2))
 F32 = jnp.float32
 BF16 = jnp.bfloat16
+F8 = jnp.float8_e4m3fn
 MESH = pl.DeviceIdType.MESH
 
 
@@ -54,11 +55,11 @@
     load_sem,
     oh_lo,
     oh_hi,
-    left,
     pieces,
     err,
     wts,
     table,
+    rows_ref,
     next_out0,
     prev_out0,
     from_prev0,
@@ -234,6 +235,11 @@
     )
     high_first = sorted(range(1, nz), key=lambda step: -min(step, nz - step))
 
+    def tree(terms):
+        while len(terms) > 1:
+            terms = [sum(terms[i : i + 2]) for i in range(0, len(terms), 2)]
+        return terms[0]
+
     def reduce_start(value):
         first_out[...] = value
         for step in far_first:
@@ -255,9 +261,7 @@
                 for pc in range(nc):
                     if step or pc != HUB:
                         first_copy(step, pc, (px * ny + py) * nc + pc).wait_recv()
-            value = first_in[0]
-            for slot in range(1, plane_size * nc):
-                value = value + first_in[slot]
+            value = tree([first_in[slot] for slot in range(plane_size * nc)])
             second_out[...] = value
             second_in[z] = value
             for step in high_first:
@@ -287,10 +291,7 @@
                 if pc != HUB:
                     second_copy(0, pc, z).wait_send()
 
-        value = second_in[0]
-        for slot in range(1, nz):
-            value = value + second_in[slot]
-        return value
+        return tree([second_in[slot] for slot in range(nz)])
 
     eye = lax.broadcasted_iota(jnp.int32, (cams, cams), 0) == lax.broadcasted_iota(
         jnp.int32, (cams, cams), 1
@@ -325,37 +326,43 @@
             running = running + first[k] * second[k]
         return jnp.sum(running, axis=0, keepdims=True)
 
-    for load in loads[:5]:
+    for load in loads:
         load.wait()
     count = stand(cnt_ref[...].astype(F32))
     guess = [stand(guess_ref[k : k + 1, :]) for k in range(9)]
     position = lax.broadcasted_iota(jnp.int32, (cams, slots), 1).astype(F32)
     wts[...] = jnp.where(position < wide(count), 1.0, 0.0)
 
-    lo_line = lax.broadcasted_iota(jnp.int32, (128, slots), 0).astype(F32).astype(BF16)
-    hi_line = lax.broadcasted_iota(jnp.int32, (16, slots), 0).astype(F32).astype(BF16)
+    lo_line = lax.broadcasted_iota(jnp.int32, (256, slots), 0).astype(F32).astype(BF16)
+    hi_line = lax.broadcasted_iota(jnp.int32, (16, slots), 0)
+    hi_line = (hi_line & 7).astype(F32).astype(BF16)
     one, none = jnp.ones((), BF16), jnp.zeros((), BF16)
     for c in range(cams):
         row = obs_ref[c : c + 1, :]
-        low = (row & 127).astype(F32)
-        high = (row >> 7).astype(F32)
+        low = ((row & 127) + ((row >> 10) << 7)).astype(F32)
+        high = ((row >> 7) & 7).astype(F32)
         here = pl.ds(c * slots, slots)
-        oh_lo[:, here] = jnp.where(spread(low, 128).astype(BF16) == lo_line, one, none)
+        hit = jnp.where(spread(low, 256).astype(BF16) == lo_line, one, none)
+        oh_lo[:, here] = hit.astype(F8)
         oh_hi[:, here] = jnp.where(spread(high, 16).astype(BF16) == hi_line, one, none)
 
-    def scatter(groups):
+    def scatter(values):
+        total = None
         for c in range(cams):
             here = pl.ds(c * slots, slots)
             mask = oh_hi[:, here]
-            for g in range(groups):
-                row = spread(pieces[g, c : c + 1, :], 16).astype(BF16)
-                left[16 * g : 16 * (g + 1), here] = row * mask
-        return lax.dot_general(
-            left[: 16 * groups, :],
-            oh_lo[...],
-            (((1,), (1,)), ((), ())),
-            preferred_element_type=F32,
-        )
+            rows = []
+            for v in range(values):
+                pair = [spread(pieces[2 * v + p, c : c + 1, :], 8) for p in range(2)]
+                rows.append(jnp.concatenate(pair, axis=0).astype(BF16) * mask)
+            part = lax.dot_general(
+                jnp.concatenate(rows, axis=0),
+                oh_lo[:, here],
+                (((1,), (1,)), ((), ())),
+                preferred_element_type=F32,
+            )
+            total = part if total is None else total + part
+        return total
 
     def cut(index, value):
         first = value.astype(BF16).astype(F32)
@@ -363,7 +370,8 @@
         pieces[2 * index + 1] = value - first
 
     def joined(result, index):
-        return result[32 * index : 32 * index + 16] + result[32 * index + 16 : 32 * index + 32]
+        both = result[16 * index : 16 * index + 8] + result[16 * index + 8 : 16 * index + 16]
+        return jnp.concatenate([both[:, :128], both[:, 128:]], axis=0)
 
     def project(vector):
         weights = wts[...]
@@ -443,17 +451,26 @@
     def finish(vector, errors, points):
         for j in range(3):
             table[j] = points[j]
-        picked = []
-        for j in range(3):
-            found = jnp.zeros((cams * tiles, 128), F32)
-            for h in range(14):
-                row = spread(table[j, h : h + 1, :], cams * tiles)
-                found = jnp.where(obs_hi == h, lane_pick(row, obs_lo), found)
-            picked.append(
-                jnp.concatenate(
-                    [found[cams * t : cams * (t + 1)] for t in range(tiles)], axis=1
-                )
+        found = [[] for _ in range(3)]
+        for block in range(cams * tiles // 8):
+            low, high = (part[8 * block : 8 * block + 8] for part in (obs_lo, obs_hi))
+            masks = [high == h for h in range(14)]
+            for j in range(3):
+                value = jnp.zeros((8, 128), F32)
+                for h in range(14):
+                    row = spread(table[j, h : h + 1, :], 8)
+                    value = jnp.where(masks[h], lane_pick(row, low), value)
+                found[j].append(value)
+        picked = [
+            jnp.concatenate(
+                [
+                    jnp.concatenate(found[j][cams // 8 * t : cams // 8 * (t + 1)], axis=0)
+                    for t in range(tiles)
+                ],
+                axis=1,
             )
+            for j in range(3)
+        ]
         weights = wts[...]
         adjusted = []
         for row in range(2):
@@ -469,8 +486,6 @@
             image.append(cam_damp * vector[k] + narrow_sum(both))
         return image
 
-    for load in loads[5:]:
-        load.wait()
     cam_damp = stand(cdamp_ref[...])
     right = [stand(rhs_ref[k : k + 1, :]) for k in range(9)]
 
@@ -481,7 +496,7 @@
         product = product + pj_ref[3 + a].astype(F32) * pj_ref[3 + b].astype(F32)
         cut(i, product * weights)
     products(6, errors)
-    result = scatter(18)
+    result = scatter(9)
     sums = []
     damping = jnp.concatenate([damp_ref[...], jnp.zeros((8, 128), F32)], axis=0)
     for i in range(9):
@@ -525,7 +540,7 @@
     def forward(vector, index):
         errors = project(vector)
         products(0, errors)
-        result = scatter(6)
+        result = scatter(3)
         sums = [joined(result, i) for i in range(3)]
         to_next, to_prev = next_out.at[index], prev_out.at[index]
         for i in range(3):
@@ -570,6 +585,12 @@
     curve_t = damped + jnp.sum(squares, axis=1, keepdims=True)
     reduce_start(jnp.where(lane == len(scalars), curve_t, row))
     img_t = finish(dir_t, errors, points)
+    flat_rows = [
+        jnp.concatenate([lie(entry) for entry in vector], axis=0)
+        for vector in (guess, dir0, dir_t, res_t, img0, img_t)
+    ]
+    for i, block in enumerate(flat_rows):
+        rows_ref[i] = block
     row = reduce_finish()
 
     def at(index):
@@ -583,14 +604,11 @@
     curve1 = step0 * step0 * curve_t - 2.0 * shift * step0 * cross_t + shift * shift * curve0
     ratio = inner1 * recip(inner0)
     step1 = inner1 * recip(curve1 - ratio * inner1 * recip(step0))
-    dir1 = [step0 * dir_t[k] - shift * dir0[k] for k in range(9)]
-    res1 = [res_t[k] - shift * img0[k] for k in range(9)]
-    img1 = [step0 * img_t[k] - shift * img0[k] for k in range(9)]
-    for k in range(9):
-        moved = guess[k] + step0 * dir0[k] + step1 * (dir1[k] + ratio * dir0[k])
-        out_ref[0, k : k + 1, :] = lie(moved)
-        left_over = res1[k] - step1 * (img1[k] + ratio * img0[k])
-        out_ref[1, k : k + 1, :] = lie(left_over)
+    first_part = (step0 + step1 * (ratio - shift))[:, :cams]
+    image_part = (shift + step1 * (ratio - shift))[:, :cams]
+    second_part = (step1 * step0)[:, :cams]
+    out_ref[0] = rows_ref[0] + first_part * rows_ref[1] + second_part * rows_ref[2]
+    out_ref[1] = rows_ref[3] - image_part * rows_ref[4] - second_part * rows_ref[5]
 
 
 def local(dims, cam_jac, point_jac, obs_point, obs_count, back_list, front_list, point_damp,
@@ -621,13 +639,13 @@
         scratch_shapes=[
             *[pltpu.VMEM(array.shape, array.dtype) for array in arrays],
             pltpu.SemaphoreType.DMA((len(arrays),)),
-            pltpu.VMEM((128, entries), BF16),
+            pltpu.VMEM((256, entries), F8),
             pltpu.VMEM((16, entries), BF16),
-            pltpu.VMEM((288, entries), BF16),
             pltpu.VMEM((18, cams, slots), F32),
             pltpu.VMEM((2, cams, slots), F32),
             pltpu.VMEM((cams, slots), F32),
             pltpu.VMEM((3, 16, 128), F32),
+            pltpu.VMEM((6, 9, cams), F32),
             pltpu.VMEM((9, 8, 128), F32),
             pltpu.VMEM((9, 8, 128), F32),
             pltpu.VMEM((9, 8, 128), F32),

time: 38.3 us -> 37.4 us (0.977)
  Pallas kernels: 37 us -> 36.1 us
    pallas_call x1, Pallas kernels: 37 us -> 36.1 us  [local(): pl.pallas_call(functools.partial(kernel, dims), out_shape=shape, in_specs...]
where the time goes in v3:
time: 37.4 us; the launch traced here: 37.3 us
  Pallas kernels  36.1 us (97%)
  between operations  0.64 us (2%)
  local copies, waits for them, and re-layouts  0.61 us (2%)
    pallas_call x1, Pallas kernels, local(): pl.pallas_call(functools.partial(kernel, dims), out_shape=shape, in_specs...  36.1 us

profile of v3, /device:TPU:1, one launch (start us, length us, event | category | flops | bytes accessed | tf_op | source)
XLA Modules:
  0.0 37.3 jit_solution(5660832248438624174)
XLA Ops:
  0.6 36.1 %shard_map.113 = f32[2,9,16]{2,1,0:T(8,128)S(1)} custom-call(bf16[18,16,512]{2,1,0:T(8,128)(2,1)} %cj_hbm.1, bf16[6,16,512]{2,1,0:T(8,128)(2,1)} %pj_hbm.1, s32[16,512]{1,0:T(8,128)} %obs_hbm.1, s32[1,16]{1,0:T(1,128)} %bitcast.8, s32[1,384]{1,0:T(1,128)} %back_hbm.1, s32[1,384]{1,0:T(1,128)} %front_hbm.1, f32[8,128]{1,0:T(8,128)} %bitcast.7, ...), custom_call_target="tpu_custom_call" | custom-call | tf_op jit(solution)/shard_map/pallas_call | solution.py:634
  36.7 0.6 %slice_bitcast_fusion = (f32[9,16]{1,0:T(8,128)}, f32[9,16]{1,0:T(8,128)}) fusion(f32[2,9,16]{2,1,0:T(8,128)S(1)} %shard_map.113), kind=kLoop, calls=%fused_computation | loop fusion | bytes 2304 | tf_op jit(solution)/shard_map/squeeze | solution.py:672

commit v4 on v3

--- a/solution.py
+++ b/solution.py
@@ -55,6 +55,8 @@
     load_sem,
     oh_lo,
     oh_hi,
+    oh_lo2,
+    oh_hi2,
     pieces,
     err,
     wts,
@@ -88,7 +90,7 @@
         (back_hbm, back_ref),
         (front_hbm, front_ref),
         (pj_hbm, pj_ref),
-        (cj_hbm, cj_ref),
+        *[(cj_hbm.at[pl.ds(6 * i, 6)], cj_ref.at[pl.ds(6 * i, 6)]) for i in range(3)],
         (damp_hbm, damp_ref),
         (cdamp_hbm, cdamp_ref),
         (rhs_hbm, rhs_ref),
@@ -197,11 +199,20 @@
         @pl.when(has_prev)
         def _():
             ahead.wait_recv()
+
+        @pl.when(has_next)
+        def _():
+            behind.wait_recv()
+
+    def border_sent(copies):
+        ahead, behind = copies
+
+        @pl.when(has_prev)
+        def _():
             behind.wait_send()
 
         @pl.when(has_next)
         def _():
-            behind.wait_recv()
             ahead.wait_send()
 
     plane_me = (x * ny + y) * nc + core
@@ -271,16 +282,22 @@
                 if pc != HUB:
                     second_copy(0, pc, z).start()
 
+        @pl.when(jnp.logical_not(hub))
+        def _():
+            second_copy(0, core, z).wait_recv()
+
+        for step in range(1, nz):
+            second_copy(step, core, height_at(step, -1)).wait_recv()
+
+        return tree([second_in[slot] for slot in range(nz)])
+
+    def reduce_sent():
         for step in far_first:
             first_copy(step, core, plane_me).wait_send()
 
         @pl.when(jnp.logical_not(hub))
         def _():
             first_copy(0, core, plane_me).wait_send()
-            second_copy(0, core, z).wait_recv()
-
-        for step in range(1, nz):
-            second_copy(step, core, height_at(step, -1)).wait_recv()
 
         @pl.when(hub)
         def _():
@@ -290,8 +307,6 @@
             for pc in range(nc):
                 if pc != HUB:
                     second_copy(0, pc, z).wait_send()
-
-        return tree([second_in[slot] for slot in range(nz)])
 
     eye = lax.broadcasted_iota(jnp.int32, (cams, cams), 0) == lax.broadcasted_iota(
         jnp.int32, (cams, cams), 1
@@ -344,10 +359,10 @@
         here = pl.ds(c * slots, slots)
         hit = jnp.where(spread(low, 256).astype(BF16) == lo_line, one, none)
         oh_lo[:, here] = hit.astype(F8)
-        oh_hi[:, here] = jnp.where(spread(high, 16).astype(BF16) == hi_line, one, none)
+        oh_hi[:, here] = jnp.where(spread(high, 16).astype(BF16) == hi_line, one if c % 2 == 0 else -one, none)
 
     def scatter(values):
-        total = None
+        halves = [None, None]
         for c in range(cams):
             here = pl.ds(c * slots, slots)
             mask = oh_hi[:, here]
@@ -361,8 +376,28 @@
                 (((1,), (1,)), ((), ())),
                 preferred_element_type=F32,
             )
-            total = part if total is None else total + part
-        return total
+            before = halves[c % 2]
+            halves[c % 2] = part if before is None else before + part
+        return halves[0] - halves[1]
+
+    def scatter_wide(values):
+        halves = [None, None]
+        for c in range(cams):
+            here = pl.ds(c * slots, slots)
+            mask = oh_hi2[:, here]
+            rows = [
+                spread(pieces[g, c : c + 1, :], 16).astype(BF16) * mask
+                for g in range(2 * values)
+            ]
+            part = lax.dot_general(
+                jnp.concatenate(rows, axis=0),
+                oh_lo2[:, here],
+                (((1,), (1,)), ((), ())),
+                preferred_element_type=F32,
+            )
+            before = halves[c % 2]
+            halves[c % 2] = part if before is None else before + part
+        return halves[0] - halves[1]
 
     def cut(index, value):
         first = value.astype(BF16).astype(F32)
@@ -513,13 +548,27 @@
         + has_next.astype(jnp.int32)
         + has_prev.astype(jnp.int32),
     )
+    sent = []
     copies = border_copies(0, next_out0, prev_out0, from_prev0, from_next0)
     border_start(copies)
+    lo_line = lax.broadcasted_iota(jnp.int32, (128, slots), 0).astype(F32).astype(BF16)
+    hi_line = lax.broadcasted_iota(jnp.int32, (16, slots), 0).astype(F32).astype(BF16)
+    one, none = jnp.ones((), BF16), jnp.zeros((), BF16)
+    for c in range(cams):
+        row = obs_ref[c : c + 1, :]
+        low = (row & 127).astype(F32)
+        high = (row >> 7).astype(F32)
+        here = pl.ds(c * slots, slots)
+        hit = jnp.where(spread(low, 128).astype(BF16) == lo_line, one, none)
+        oh_lo2[:, here] = hit.astype(F8)
+        oh_hi2[:, here] = jnp.where(spread(high, 16).astype(BF16) == hi_line, one if c % 2 == 0 else -one, none)
+
     precond = []
     for k in range(9):
         square = cj_ref[k].astype(F32) ** 2 + cj_ref[9 + k].astype(F32) ** 2
         precond.append(recip(cam_damp + narrow_sum(square * weights)))
     border_wait(copies)
+    sent.append(copies)
     sums = [complete(sums[i], from_prev0[i], from_next0[i]) for i in range(9)]
     ent = sums[:6]
     cofactors = [
@@ -540,8 +589,10 @@
     def forward(vector, index):
         errors = project(vector)
         products(0, errors)
-        result = scatter(3)
-        sums = [joined(result, i) for i in range(3)]
+        result = scatter_wide(3)
+        sums = [
+            result[32 * i : 32 * i + 16] + result[32 * i + 16 : 32 * i + 32] for i in range(3)
+        ]
         to_next, to_prev = next_out.at[index], prev_out.at[index]
         for i in range(3):
             outgoing(sums[i], i, to_next, to_prev)
@@ -558,6 +609,7 @@
 
     errors, sums, copies = forward(dir0, 0)
     border_wait(copies)
+    sent.append(copies)
     sums = arrived(0, sums)
     img0 = finish(dir0, errors, solve(sums, inverse))
     res_t = [res0[k] - img0[k] for k in range(9)]
@@ -578,6 +630,7 @@
     squares = jnp.sum(squares, axis=0, keepdims=True)
     squares = sum(squares[:, 128 * t : 128 * (t + 1)] for t in range(tiles))
     border_wait(copies)
+    sent.append(copies)
     sums = arrived(1, sums)
     points = solve(sums, inverse)
     energy = sum(sums[j][:8] * points[j][:8] for j in range(3))
@@ -591,6 +644,8 @@
     ]
     for i, block in enumerate(flat_rows):
         rows_ref[i] = block
+    for copies in sent:
+        border_sent(copies)
     row = reduce_finish()
 
     def at(index):
@@ -609,6 +664,7 @@
     second_part = (step1 * step0)[:, :cams]
     out_ref[0] = rows_ref[0] + first_part * rows_ref[1] + second_part * rows_ref[2]
     out_ref[1] = rows_ref[3] - image_part * rows_ref[4] - second_part * rows_ref[5]
+    reduce_sent()
 
 
 def local(dims, cam_jac, point_jac, obs_point, obs_count, back_list, front_list, point_damp,
@@ -638,8 +694,10 @@
         out_specs=vmem,
         scratch_shapes=[
             *[pltpu.VMEM(array.shape, array.dtype) for array in arrays],
-            pltpu.SemaphoreType.DMA((len(arrays),)),
+            pltpu.SemaphoreType.DMA((len(arrays) + 2,)),
             pltpu.VMEM((256, entries), F8),
+            pltpu.VMEM((16, entries), BF16),
+            pltpu.VMEM((128, entries), F8),
             pltpu.VMEM((16, entries), BF16),
             pltpu.VMEM((18, cams, slots), F32),
             pltpu.VMEM((2, cams, slots), F32),

time: 37.4 us -> 36.4 us (0.973)
  Pallas kernels: 36.1 us -> 35 us
    pallas_call x1, Pallas kernels: 36.1 us -> 35 us  [local(): pl.pallas_call(functools.partial(kernel, dims), out_shape=shape, in_specs...]
where the time goes in v4:
time: 36.4 us; the launch traced here: 36.3 us
  Pallas kernels  35 us (96%)
  between operations  0.64 us (2%)
  local copies, waits for them, and re-layouts  0.61 us (2%)
    pallas_call x1, Pallas kernels, local(): pl.pallas_call(functools.partial(kernel, dims), out_shape=shape, in_specs...  35 us

profile of v4, /device:TPU:1, one launch (start us, length us, event | category | flops | bytes accessed | tf_op | source)
XLA Modules:
  0.0 36.3 jit_solution(98600183801762934)
XLA Ops:
  0.6 35.0 %shard_map.113 = f32[2,9,16]{2,1,0:T(8,128)S(1)} custom-call(bf16[18,16,512]{2,1,0:T(8,128)(2,1)} %cj_hbm.1, bf16[6,16,512]{2,1,0:T(8,128)(2,1)} %pj_hbm.1, s32[16,512]{1,0:T(8,128)} %obs_hbm.1, s32[1,16]{1,0:T(1,128)} %bitcast.8, s32[1,384]{1,0:T(1,128)} %back_hbm.1, s32[1,384]{1,0:T(1,128)} %front_hbm.1, f32[8,128]{1,0:T(8,128)} %bitcast.7, ...), custom_call_target="tpu_custom_call" | custom-call | tf_op jit(solution)/shard_map/pallas_call | solution.py:690
  35.6 0.6 %slice_bitcast_fusion = (f32[9,16]{1,0:T(8,128)}, f32[9,16]{1,0:T(8,128)}) fusion(f32[2,9,16]{2,1,0:T(8,128)S(1)} %shard_map.113), kind=kLoop, calls=%fused_computation | loop fusion | bytes 2304 | tf_op jit(solution)/shard_map/squeeze | solution.py:730

commit v5 on v4

--- a/solution.py
+++ b/solution.py
@@ -451,25 +451,34 @@
     ).astype(jnp.int32)
     place_lo, place_hi = places[:8], places[8:16] - 1
 
+    def choose(options, bits):
+        for bit in bits:
+            options = [
+                jnp.where(bit, options[i + 1], options[i]) if i + 1 < len(options) else options[i]
+                for i in range(0, len(options), 2)
+            ]
+        return options[0]
+
+    list_bits = [(list_hi & (1 << b)) != 0 for b in range(3)]
+    place_bits = [(place_hi & (1 << b)) != 0 for b in range(3)]
     sub8 = lax.broadcasted_iota(jnp.int32, (8, 128), 0)
     back_rows = sub8 < 3
 
     def outgoing(sums, index, to_next, to_prev):
         own, outer = sums[:8], sums[8:16]
-        picked = jnp.zeros((8, 128), F32)
-        for h in range(8):
-            found = lane_pick(spread(own[h : h + 1], 8), list_lo)
-            picked = jnp.where(list_hi == h, found, picked)
+        picked = choose(
+            [lane_pick(spread(own[h : h + 1], 8), list_lo) for h in range(8)], list_bits
+        )
         to_next[index] = jnp.where(back_rows, picked, outer)
         to_prev[index] = jnp.where(back_rows, outer, picked)
 
     def complete(sums, prev_block, next_block):
         own, outer = sums[:8], sums[8:16]
         mixed = jnp.where(back_rows, next_block, prev_block)
-        added = jnp.zeros((8, 128), F32)
-        for h in range(6):
-            found = lane_pick(spread(mixed[h : h + 1], 8), place_lo)
-            added = jnp.where(place_hi == h, found, added)
+        added = choose(
+            [lane_pick(spread(mixed[h : h + 1], 8), place_lo) for h in range(6)], place_bits
+        )
+        added = jnp.where(place_hi >= 0, added, 0.0)
         return jnp.concatenate(
             [own + added, outer + jnp.where(back_rows, prev_block, next_block)], axis=0
         )
@@ -489,13 +498,14 @@
         found = [[] for _ in range(3)]
         for block in range(cams * tiles // 8):
             low, high = (part[8 * block : 8 * block + 8] for part in (obs_lo, obs_hi))
-            masks = [high == h for h in range(14)]
+            bits = [(high & (1 << b)) != 0 for b in range(4)]
             for j in range(3):
-                value = jnp.zeros((8, 128), F32)
-                for h in range(14):
-                    row = spread(table[j, h : h + 1, :], 8)
-                    value = jnp.where(masks[h], lane_pick(row, low), value)
-                found[j].append(value)
+                found[j].append(
+                    choose(
+                        [lane_pick(spread(table[j, h : h + 1, :], 8), low) for h in range(14)],
+                        bits,
+                    )
+                )
         picked = [
             jnp.concatenate(
                 [

time: 36.4 us -> 35.9 us (0.986)
  Pallas kernels: 35 us -> 34.5 us
    pallas_call x1, Pallas kernels: 35 us -> 34.5 us  [local(): pl.pallas_call(functools.partial(kernel, dims), out_shape=shape, in_specs...]
where the time goes in v5:
time: 35.9 us; the launch traced here: 35.8 us
  Pallas kernels  34.5 us (96%)
  between operations  0.64 us (2%)
  local copies, waits for them, and re-layouts  0.61 us (2%)
    pallas_call x1, Pallas kernels, local(): pl.pallas_call(functools.partial(kernel, dims), out_shape=shape, in_specs...  34.5 us

profile of v5, /device:TPU:1, one launch (start us, length us, event | category | flops | bytes accessed | tf_op | source)
XLA Modules:
  0.0 35.8 jit_solution(14461418901184014780)
XLA Ops:
  0.6 34.5 %shard_map.113 = f32[2,9,16]{2,1,0:T(8,128)S(1)} custom-call(bf16[18,16,512]{2,1,0:T(8,128)(2,1)} %cj_hbm.1, bf16[6,16,512]{2,1,0:T(8,128)(2,1)} %pj_hbm.1, s32[16,512]{1,0:T(8,128)} %obs_hbm.1, s32[1,16]{1,0:T(1,128)} %bitcast.8, s32[1,384]{1,0:T(1,128)} %back_hbm.1, s32[1,384]{1,0:T(1,128)} %front_hbm.1, f32[8,128]{1,0:T(8,128)} %bitcast.7, ...), custom_call_target="tpu_custom_call" | custom-call | tf_op jit(solution)/shard_map/pallas_call | solution.py:700
  35.2 0.6 %slice_bitcast_fusion = (f32[9,16]{1,0:T(8,128)}, f32[9,16]{1,0:T(8,128)}) fusion(f32[2,9,16]{2,1,0:T(8,128)S(1)} %shard_map.113), kind=kLoop, calls=%fused_computation | loop fusion | bytes 2304 | tf_op jit(solution)/shard_map/squeeze | solution.py:740

commit v6 on v5

--- a/solution.py
+++ b/solution.py
@@ -165,16 +165,16 @@
 
     def border_copies(index, to_next, to_prev, came_prev, came_next):
         ahead = pltpu.make_async_remote_copy(
-            src_ref=to_next,
-            dst_ref=came_prev,
+            src_ref=to_next.at[:, pl.ds(0, 6)],
+            dst_ref=came_prev.at[:, pl.ds(0, 6)],
             send_sem=ex_send.at[index, 0],
             recv_sem=ex_recv.at[index, 0],
             device_id=(jnp.minimum(me + 1, total - 1),),
             device_id_type=MESH,
         )
         behind = pltpu.make_async_remote_copy(
-            src_ref=to_prev,
-            dst_ref=came_next,
+            src_ref=to_prev.at[:, pl.ds(0, 6)],
+            dst_ref=came_next.at[:, pl.ds(0, 6)],
             send_sem=ex_send.at[index, 1],
             recv_sem=ex_recv.at[index, 1],
             device_id=(jnp.maximum(me - 1, 0),),
@@ -474,6 +474,8 @@
 
     def complete(sums, prev_block, next_block):
         own, outer = sums[:8], sums[8:16]
+        prev_block = jnp.where(sub8 < 6, prev_block, 0.0)
+        next_block = jnp.where(sub8 < 6, next_block, 0.0)
         mixed = jnp.where(back_rows, next_block, prev_block)
         added = choose(
             [lane_pick(spread(mixed[h : h + 1], 8), place_lo) for h in range(6)], place_bits
@@ -668,7 +670,7 @@
     inner1 = inner_t - 2.0 * shift * cross_t + shift * shift * (curve0 - cross_t)
     curve1 = step0 * step0 * curve_t - 2.0 * shift * step0 * cross_t + shift * shift * curve0
     ratio = inner1 * recip(inner0)
-    step1 = inner1 * recip(curve1 - ratio * inner1 * recip(step0))
+    step1 = inner1 * recip(curve1 - ratio * inner1 * (curve0 * recip(curve0 + mixed_t)))
     first_part = (step0 + step1 * (ratio - shift))[:, :cams]
     image_part = (shift + step1 * (ratio - shift))[:, :cams]
     second_part = (step1 * step0)[:, :cams]

time: 35.9 us -> 35.7 us (level)
  no operation moved by 1% of the time
where the time goes in v6:
time: 35.7 us; the launch traced here: 35.6 us
  Pallas kernels  34.3 us (96%)
  between operations  0.64 us (2%)
  local copies, waits for them, and re-layouts  0.61 us (2%)
    pallas_call x1, Pallas kernels, local(): pl.pallas_call(functools.partial(kernel, dims), out_shape=shape, in_specs...  34.3 us

profile of v6, /device:TPU:1, one launch (start us, length us, event | category | flops | bytes accessed | tf_op | source)
XLA Modules:
  0.0 35.6 jit_solution(8355077514622353349)
XLA Ops:
  0.6 34.3 %shard_map.113 = f32[2,9,16]{2,1,0:T(8,128)S(1)} custom-call(bf16[18,16,512]{2,1,0:T(8,128)(2,1)} %cj_hbm.1, bf16[6,16,512]{2,1,0:T(8,128)(2,1)} %pj_hbm.1, s32[16,512]{1,0:T(8,128)} %obs_hbm.1, s32[1,16]{1,0:T(1,128)} %bitcast.8, s32[1,384]{1,0:T(1,128)} %back_hbm.1, s32[1,384]{1,0:T(1,128)} %front_hbm.1, f32[8,128]{1,0:T(8,128)} %bitcast.7, ...), custom_call_target="tpu_custom_call" | custom-call | tf_op jit(solution)/shard_map/pallas_call | solution.py:702
  35.0 0.6 %slice_bitcast_fusion = (f32[9,16]{1,0:T(8,128)}, f32[9,16]{1,0:T(8,128)}) fusion(f32[2,9,16]{2,1,0:T(8,128)S(1)} %shard_map.113), kind=kLoop, calls=%fused_computation | loop fusion | bytes 2304 | tf_op jit(solution)/shard_map/squeeze | solution.py:742
